TPU v7x, 32 devices: a whole 2x2x4 slice. The times are simulated.
32 devices in a mesh: aa: 8 (over y, x, core), ba: 4 (over z).
Axes of the slice: x: 2, y: 2, z: 4, core: 2. Of those that a mesh axis runs over, the one named last changes fastest.
Arguments:
- queries: bfloat16 [4, 128, 8192], P('ba', None, 'aa'), may hold values from -10 to 10
- new_kv: bfloat16 [4, 128, 2, 512], P('ba', 'aa'), may hold values from -4 to 4
- pool: bfloat16 [4, 64, 32, 2, 512], P('ba', 'aa'), may hold values from -4 to 4
- page_table: int32 [4, 32], P('ba', 'aa'), may hold values from 0 to 7, as said below
- ctx_len: int32 [4, 8], P('ba', 'aa'), may hold values from 1 to 128, as said below
- move_page: int32 [4, 24], P('ba', 'aa'), may hold values from 0 to 7, as said below
- move_dest: int32 [4, 24], P('ba', 'aa'), may hold values from 0 to 3, as said below
- append_page: int32 [4, 8], P('ba', 'aa'), may hold values from 0 to 7
Outputs:
- attended: bfloat16 [4, 128, 8192], P('ba', None, 'aa')
- pool_out: bfloat16 [4, 64, 32, 2, 512], P('ba', 'aa')
Inputs may be any that keep to these rules, and one draw needn't show every extreme that they name: `page_table`: the entries of one device are distinct pages of its pool and differ from its leaving pages and its append page. `ctx_len`: for each instance some index of aa holds exactly 128 live rows. `move_page`: the 3 entries of one device are distinct pages of its pool. `move_dest`: A device never names its own instance and names any one instance at most 2 times; for each index of aa one instance is named exactly 2 times by the device of every other instance.
All inputs are finite; a program needn't handle non-finite values.
Results may differ from a plain program's by a relative error of at most 0.0017.
Values may be sent and summed in bfloat16 or wider, within the bound.
A program may use at most 64 MiB of HBM per device.

v0:
```python
import functools
import math

import jax
import jax.numpy as jnp
from jax import lax
from jax.experimental import pallas as pl
from jax.experimental.pallas import tpu as pltpu
from jax.sharding import PartitionSpec as P

HEAD_DIM = 128
MOST = 2
LANES = 128
BLOCK = 256
NEG_LARGE = -1e30
MESH = pl.DeviceIdType.MESH


def kernel(
    n_inst, n_aa, kv_heads,
    table_ref, len_ref, page_ref, dest_ref, q_ref, pool_ref, fresh_ref,
    out_ref,
    st_res, st_new, st_mov, st_len, st_occ,
    kv_res, kv_new, kv_mov, len_all, occ_all,
    run_max, run_sum, run_out, q_turned,
    s_res, r_res, s_new, r_new, s_mov, r_mov, s_len, r_len, s_occ, r_occ,
    fs_res, fr_res, fs_new, fr_new, fs_mov, fr_mov, fs_len, fr_len, fs_occ, fr_occ,
    l_new, l_res,
):
    b = lax.axis_index("ba")
    a = lax.axis_index("aa")
    share = n_aa // kv_heads
    mine, member = a // share, a % share
    table = table_ref.shape[1]
    moves = page_ref.shape[1]
    page_rows = pool_ref.shape[1]
    queries = q_ref.shape[0]
    heads = q_ref.shape[1] // HEAD_DIM

    def inst(r):
        return lax.rem(b + r + n_inst, n_inst)

    def at_head(j):
        return lax.rem(mine + j + kv_heads, kv_heads) * share + member

    def peer(k):
        return mine * share + lax.rem(member + k + share, share)

    barrier = pltpu.get_barrier_semaphore()
    partners = [(r, j) for r in range(n_inst) for j in range(kv_heads) if r or j]
    for r, j in partners:
        pl.semaphore_signal(barrier, inc=1, device_id={"ba": inst(r), "aa": at_head(j)}, device_id_type=MESH)
    for k in range(1, share):
        pl.semaphore_signal(barrier, inc=1, device_id={"ba": b, "aa": peer(k)}, device_id_type=MESH)

    spots = [(h, w) for h in range(kv_heads) for w in range(2)]

    def columns_of(h):
        return slice(h * HEAD_DIM, (h + 1) * HEAD_DIM)

    line = lax.broadcasted_iota(jnp.int32, (8, LANES), 0)
    for r in range(1, n_inst):
        target = inst(r)
        slot_bias = []
        for m in range(MOST):
            chosen, occupied, seen = jnp.int32(0), jnp.int32(0), jnp.int32(0)
            for i in range(moves):
                hit = (dest_ref[0, i] == target).astype(jnp.int32)
                here = hit * (seen == m).astype(jnp.int32)
                chosen = chosen + here * page_ref[0, i]
                occupied = occupied + here
                seen = seen + hit
            for h, w in spots:
                st_mov[r - 1, h, w, m * page_rows:(m + 1) * page_rows, :] = pool_ref[chosen, :, w, columns_of(h)]
            slot_bias.append(jnp.where(occupied > 0, 0.0, NEG_LARGE))
        row = jnp.full((8, LANES), slot_bias[0], jnp.float32)
        for m in range(1, MOST):
            row = jnp.where(line == m, slot_bias[m], row)
        st_occ[r - 1] = row
    for j in range(table):
        for h, w in spots:
            st_res[h, w, j * page_rows:(j + 1) * page_rows, :] = pool_ref[table_ref[0, j], :, w, columns_of(h)]
    for h, w in spots:
        st_new[h, w] = fresh_ref[:, w, columns_of(h)]
    st_len[...] = jnp.full(st_len.shape, len_ref[0, 0], jnp.int32)
    len_all[a] = st_len[...]
    for h in range(heads):
        q_turned[:, h * queries:(h + 1) * queries] = q_ref[:, h * HEAD_DIM:(h + 1) * HEAD_DIM].T

    pl.semaphore_wait(barrier, len(partners) + share - 1)

    def remote(src, dst, ss, rs, ba, aa):
        return pltpu.make_async_remote_copy(
            src_ref=src, dst_ref=dst, send_sem=ss, recv_sem=rs,
            device_id={"ba": ba, "aa": aa}, device_id_type=MESH,
        )

    sent = []

    def start(*args):
        c = remote(*args)
        c.start()
        sent.append(c)

    for r in range(1, n_inst):
        for j in range(kv_heads):
            to = at_head(j)
            h = lax.rem(mine + j, kv_heads)
            start(st_mov.at[r - 1, h], kv_mov.at[r - 1, member, mine], s_mov.at[r - 1, j], r_mov.at[r - 1, j], inst(r), to)
            start(st_occ.at[r - 1], occ_all.at[r - 1, member, mine], s_occ.at[r - 1, j], r_occ.at[r - 1, j], inst(r), to)
        if r == 1:
            for j in range(1, kv_heads):
                to = at_head(j)
                h = lax.rem(mine + j, kv_heads)
                start(st_new.at[h], kv_new.at[a], s_new.at[j], r_new.at[j], b, to)
                start(st_len, len_all.at[a], s_len.at[j], r_len.at[j], b, to)
                start(st_res.at[h], kv_res.at[a], s_res.at[j], r_res.at[j], b, to)
            for k in range(1, share):
                to = peer(k)
                start(st_new.at[mine], kv_new.at[a], fs_new.at[k - 1, 0], fr_new.at[k - 1, 0], b, to)
                start(st_len, len_all.at[a], fs_len.at[k - 1, 0], fr_len.at[k - 1, 0], b, to)
                start(st_res.at[mine], kv_res.at[a], fs_res.at[k - 1, 0], fr_res.at[k - 1, 0], b, to)
    own_new = pltpu.make_async_copy(st_new.at[mine], kv_new.at[a], l_new)
    own_new.start()
    own_res = pltpu.make_async_copy(st_res.at[mine], kv_res.at[a], l_res)
    own_res.start()

    def arrived(slot, rs, ss):
        remote(slot, slot, ss, rs, b, a).wait_recv()

    def relay(slot, rs, ss, fs, fr, j):
        arrived(slot, rs, ss)
        for k in range(1, share):
            start(slot, slot, fs.at[k - 1, j], fr.at[k - 1, j], b, peer(k))

    def peers_done(buf, fs, fr, first=0):
        for k in range(1, share):
            for j in range(kv_heads):
                src = lax.rem(mine - j + kv_heads, kv_heads) * share + lax.rem(member - k + share, share)
                arrived(buf.at[src], fr.at[k - 1, j], fs.at[k - 1, j])

    for j in range(1, kv_heads):
        src = at_head(-j)
        relay(kv_new.at[src], r_new.at[j], s_new.at[j], fs_new, fr_new, j)
        relay(len_all.at[src], r_len.at[j], s_len.at[j], fs_len, fr_len, j)
        relay(kv_res.at[src], r_res.at[j], s_res.at[j], fs_res, fr_res, j)

    scale = math.log2(math.e) / math.sqrt(HEAD_DIM)

    def attend(keys, values, bias, first):
        turned = values.T
        copies = BLOCK // bias.shape[1]
        wide = jnp.concatenate([bias] * copies, axis=1) if copies > 1 else bias
        for start_at in range(0, heads * queries, BLOCK):
            block = slice(start_at, start_at + BLOCK)
            s = jnp.dot(keys, q_turned[:, block], preferred_element_type=jnp.float32)
            s = s * scale + wide
            top = jnp.max(s, axis=0, keepdims=True)
            if not first:
                old = run_max[:, block]
                top = jnp.maximum(old, top)
            w = jnp.exp2(s - top)
            total = jnp.sum(w, axis=0, keepdims=True)
            high = w.astype(jnp.bfloat16)
            low = (w - high.astype(jnp.float32)).astype(jnp.bfloat16)
            out = jnp.dot(turned, high, preferred_element_type=jnp.float32)
            out = out + jnp.dot(turned, low, preferred_element_type=jnp.float32)
            if not first:
                shrink = jnp.exp2(old - top)
                total = total + run_sum[:, block] * shrink
                out = out + run_out[:, block] * shrink
            run_max[:, block] = top
            run_sum[:, block] = total
            run_out[:, block] = out

    own_new.wait()
    peers_done(kv_new, fs_new, fr_new)
    rows = lax.broadcasted_iota(jnp.int32, (queries, queries), 0)
    columns = lax.broadcasted_iota(jnp.int32, (queries, queries), 1)
    attend(
        kv_new[:, 0].reshape(-1, HEAD_DIM),
        kv_new[:, 1].reshape(-1, HEAD_DIM),
        jnp.where(rows <= columns, 0.0, NEG_LARGE),
        True,
    )
    own_res.wait()
    place = lax.broadcasted_iota(jnp.int32, (table * page_rows, LANES), 0)
    peers_done(len_all, fs_len, fr_len)
    peers_done(kv_res, fs_res, fr_res)
    def attend_resident():
        attend(
            kv_res[:, 0].reshape(-1, HEAD_DIM),
            kv_res[:, 1].reshape(-1, HEAD_DIM),
            jnp.concatenate([jnp.where(place < len_all[i, 0:1, :], 0.0, NEG_LARGE) for i in range(n_aa)], axis=0),
            False,
        )

    far = n_inst - 1

    def back(j):
        return lax.rem(mine - j + kv_heads, kv_heads)

    def other(k):
        return lax.rem(member - k + share, share)

    def relay_moved(r):
        for j in range(kv_heads):
            relay(kv_mov.at[r - 1, member, back(j)], r_mov.at[r - 1, j], s_mov.at[r - 1, j], fs_mov.at[r - 1], fr_mov.at[r - 1], j)
            relay(occ_all.at[r - 1, member, back(j)], r_occ.at[r - 1, j], s_occ.at[r - 1, j], fs_occ.at[r - 1], fr_occ.at[r - 1], j)

    def moved_from(r, k):
        for j in range(kv_heads):
            arrived(kv_mov.at[r - 1, other(k), back(j)], fr_mov.at[r - 1, k - 1, j], fs_mov.at[r - 1, k - 1, j])
            arrived(occ_all.at[r - 1, other(k), back(j)], fr_occ.at[r - 1, k - 1, j], fs_occ.at[r - 1, k - 1, j])

    def attend_moved(r, members):
        attend(
            jnp.concatenate([kv_mov[r - 1, i, :, 0].reshape(-1, HEAD_DIM) for i in members], axis=0),
            jnp.concatenate([kv_mov[r - 1, i, :, 1].reshape(-1, HEAD_DIM) for i in members], axis=0),
            jnp.concatenate([
                jnp.broadcast_to(occ_all[r - 1, i, c, m:m + 1, :], (page_rows, LANES))
                for i in members for c in range(kv_heads) for m in range(MOST)
            ], axis=0),
            False,
        )

    relay_moved(1)
    attend_resident()
    for r in range(1, far):
        if r + 1 < far:
            relay_moved(r + 1)
        for k in range(1, share):
            moved_from(r, k)
        attend_moved(r, range(share))
    if far > 1:
        relay_moved(far)
    attend_moved(far, [member])
    for k in range(1, share):
        moved_from(far, k)
        attend_moved(far, [other(k)])

    def turn(h):
        part = slice(h * queries, (h + 1) * queries)
        return (run_out[:, part] / run_sum[:, part]).T

    for h in range(heads):
        out_ref[:, h * HEAD_DIM:(h + 1) * HEAD_DIM] = turn(h).astype(out_ref.dtype)
    for c in sent:
        c.wait_send()


def finish(append_ref, rows_ref, pool_ref, fresh_ref, out_ref, updated_ref):
    out_ref[...] = rows_ref[...]
    updated_ref[...] = pool_ref[...]
    updated_ref[append_ref[0, 0], 0:fresh_ref.shape[0]] = fresh_ref[...]


def local(n_inst, n_aa, queries, new_kv, pool, page_table, ctx_len, move_page, move_dest, append_page):
    pool_pages = pool[0]
    pages, page_rows, _, width = pool_pages.shape
    kv_heads = width // HEAD_DIM
    share = n_aa // kv_heads
    fresh_rows = new_kv[0]
    fresh_count = fresh_rows.shape[0]
    query_count, q_width = queries.shape[1:]
    heads = q_width // HEAD_DIM
    table = page_table.shape[1]
    far = n_inst - 1
    bf, f32 = jnp.bfloat16, jnp.float32
    dma = pltpu.SemaphoreType.DMA
    near = [dma((kv_heads,))] * 4
    attended = pl.pallas_call(
        functools.partial(kernel, n_inst, n_aa, kv_heads),
        out_shape=jax.ShapeDtypeStruct((query_count, q_width), bf),
        in_specs=[pl.BlockSpec(memory_space=pltpu.SMEM)] * 4 + [pl.BlockSpec(memory_space=pltpu.VMEM)] * 3,
        out_specs=pl.BlockSpec(memory_space=pltpu.VMEM),
        scratch_shapes=[
            pltpu.VMEM((kv_heads, 2, table * page_rows, HEAD_DIM), bf),
            pltpu.VMEM((kv_heads, 2, fresh_count, HEAD_DIM), bf),
            pltpu.VMEM((far, kv_heads, 2, MOST * page_rows, HEAD_DIM), bf),
            pltpu.VMEM((8, LANES), jnp.int32),
            pltpu.VMEM((far, 8, LANES), f32),
            pltpu.VMEM((n_aa, 2, table * page_rows, HEAD_DIM), bf),
            pltpu.VMEM((n_aa, 2, fresh_count, HEAD_DIM), bf),
            pltpu.VMEM((far, share, kv_heads, 2, MOST * page_rows, HEAD_DIM), bf),
            pltpu.VMEM((n_aa, 8, LANES), jnp.int32),
            pltpu.VMEM((far, share, kv_heads, 8, LANES), f32),
            pltpu.VMEM((1, heads * query_count), f32),
            pltpu.VMEM((1, heads * query_count), f32),
            pltpu.VMEM((HEAD_DIM, heads * query_count), f32),
            pltpu.VMEM((HEAD_DIM, heads * query_count), bf),
            *near,
            dma((far, kv_heads)), dma((far, kv_heads)),
            dma((kv_heads,)), dma((kv_heads,)),
            dma((far, kv_heads)), dma((far, kv_heads)),
            *([dma((share - 1, kv_heads))] * 4),
            dma((far, share - 1, kv_heads)), dma((far, share - 1, kv_heads)),
            dma((share - 1, kv_heads)), dma((share - 1, kv_heads)),
            dma((far, share - 1, kv_heads)), dma((far, share - 1, kv_heads)),
            dma, dma,
        ],
        compiler_params=pltpu.CompilerParams(collective_id=0, has_side_effects=True, vmem_limit_bytes=32 * 2**20),
        name="paged_attention",
    )(page_table, ctx_len, move_page, move_dest, queries[0], pool_pages, fresh_rows)
    attended, updated = pl.pallas_call(
        finish,
        out_shape=(
            jax.ShapeDtypeStruct(attended.shape, bf),
            jax.ShapeDtypeStruct(pool_pages.shape, bf),
        ),
        in_specs=[pl.BlockSpec(memory_space=pltpu.SMEM)] + [pl.BlockSpec(memory_space=pltpu.VMEM)] * 3,
        out_specs=(pl.BlockSpec(memory_space=pltpu.VMEM),) * 2,
        compiler_params=pltpu.CompilerParams(vmem_limit_bytes=12 * 2**20),
        name="finish",
    )(append_page, attended, pool_pages, fresh_rows)
    return (attended[None], updated[None])


def solution(mesh):
    return jax.shard_map(
        functools.partial(local, mesh.shape["ba"], mesh.shape["aa"]),
        mesh=mesh,
        in_specs=(
            P("ba", None, "aa"),
            P("ba", "aa", None, None),
            P("ba", "aa", None, None, None),
            P("ba", "aa"),
            P("ba", "aa"),
            P("ba", "aa"),
            P("ba", "aa"),
            P("ba", "aa"),
        ),
        out_specs=(P("ba", None, "aa"), P("ba", "aa", None, None, None)),
        check_vma=False,
    )
```

profile of v0, /device:TPU:0, one launch (start us, length us, event | category | flops | bytes accessed | tf_op | source)
XLA Modules:
  0.0 31.8 jit_solution(1465323169411387150)
XLA Ops:
  1.9 0.0 copy-start.3
  1.9 0.0 copy-start.4
  1.9 0.0 copy-start.5
  2.0 0.6 %copy-done.3 = s32[1,4]{1,0:T(1,128)S(1)} copy-done((s32[1,4]{1,0:T(1,128)S(1)}, s32[1,4]{1,0:T(1,128)}, u32[]{:S(2)}) %copy-start.3) | copy-done | bytes 40
  2.6 0.0 copy-done.4
  2.6 0.0 copy-done.5
  2.6 0.0 copy-start
  2.6 1.0 %copy-done = bf16[1,8,32,2,512]{4,3,2,1,0:T(2,128)(2,1)S(1)} copy-done((bf16[1,8,32,2,512]{4,3,2,1,0:T(2,128)(2,1)S(1)}, bf16[1,8,32,2,512]{4,3,2,1,0:T(2,128)(2,1)}, u32[]{:S(2)}) %copy-start) | copy-done | bytes 524312
  3.7 0.0 copy-start.1
  3.7 0.9 %copy-done.1 = bf16[1,128,1024]{2,1,0:T(8,128)(2,1)S(1)} copy-done((bf16[1,128,1024]{2,1,0:T(8,128)(2,1)S(1)}, bf16[1,128,1024]{2,1,0:T(8,128)(2,1)}, u32[]{:S(2)}) %copy-start.1) | copy-done | bytes 262168
  4.6 0.0 copy-start.2
  4.6 0.8 %copy-done.2 = bf16[1,16,2,512]{3,2,1,0:T(2,128)(2,1)S(1)} copy-done((bf16[1,16,2,512]{3,2,1,0:T(2,128)(2,1)S(1)}, bf16[1,16,2,512]{3,2,1,0:T(2,128)(2,1)}, u32[]{:S(2)}) %copy-start.2) | copy-done | bytes 32792
  5.4 25.5 %paged_attention.1.rows_ref = bf16[128,1024]{1,0:T(8,128)(2,1)S(1)} custom-call(s32[1,4]{1,0:T(1,128)S(1)} %copy-done.3, s32[1,1]{1,0:T(1,128)S(6)} %copy.10.len_ref, s32[1,3]{1,0:T(1,128)S(1)} %copy-done.4, s32[1,3]{1,0:T(1,128)S(1)} %copy-done.5, bf16[128,1024]{1,0:T(8,128)(2,1)S(1)} %bitcast.7, bf16[8,32,2,512]{3,2,1,0:T(2,128)(2,1)S(1)} %bitcast.5, ...), custom_call_target="tpu_custom_call" | custom-call | tf_op jit(solution)/shard_map/paged_attention/pallas_call | solution.py:272
  30.9 0.9 %finish.1 = (bf16[128,1024]{1,0:T(8,128)(2,1)}, bf16[8,32,2,512]{3,2,1,0:T(2,128)(2,1)}) custom-call(s32[1,1]{1,0:T(1,128)S(6)} %copy.11.append_ref, bf16[128,1024]{1,0:T(8,128)(2,1)S(1)} %paged_attention.1.rows_ref, bf16[8,32,2,512]{3,2,1,0:T(2,128)(2,1)S(1)} %bitcast.6, bf16[16,2,512]{2,1,0:T(2,128)(2,1)S(1)} %bitcast.9), custom_call_target="tpu_custom_call" | custom-call | tf_op jit(solution)/shard_map/finish/pallas_call | solution.py:305
Async XLA Ops:
  1.9 0.7 %copy-start.3 = (s32[1,4]{1,0:T(1,128)S(1)}, s32[1,4]{1,0:T(1,128)}, u32[]{:S(2)}) copy-start(s32[1,4]{1,0:T(1,128)} %table_ref.1) | copy-start | bytes 52
  1.9 0.7 %copy-start.4 = (s32[1,3]{1,0:T(1,128)S(1)}, s32[1,3]{1,0:T(1,128)}, u32[]{:S(2)}) copy-start(s32[1,3]{1,0:T(1,128)} %page_ref.1) | copy-start | bytes 40
  1.9 0.7 %copy-start.5 = (s32[1,3]{1,0:T(1,128)S(1)}, s32[1,3]{1,0:T(1,128)}, u32[]{:S(2)}) copy-start(s32[1,3]{1,0:T(1,128)} %dest_ref.1) | copy-start | bytes 40
  2.6 1.0 %copy-start = (bf16[1,8,32,2,512]{4,3,2,1,0:T(2,128)(2,1)S(1)}, bf16[1,8,32,2,512]{4,3,2,1,0:T(2,128)(2,1)}, u32[]{:S(2)}) copy-start(bf16[1,8,32,2,512]{4,3,2,1,0:T(2,128)(2,1)} %param.10) | copy-start | bytes 1572868
  3.7 0.9 %copy-start.1 = (bf16[1,128,1024]{2,1,0:T(8,128)(2,1)S(1)}, bf16[1,128,1024]{2,1,0:T(8,128)(2,1)}, u32[]{:S(2)}) copy-start(bf16[1,128,1024]{2,1,0:T(8,128)(2,1)} %param.8) | copy-start | bytes 786436
  4.6 0.8 %copy-start.2 = (bf16[1,16,2,512]{3,2,1,0:T(2,128)(2,1)S(1)}, bf16[1,16,2,512]{3,2,1,0:T(2,128)(2,1)}, u32[]{:S(2)}) copy-start(bf16[1,16,2,512]{3,2,1,0:T(2,128)(2,1)} %param.9) | copy-start | bytes 98308
where the time goes:
time: 32.1 us; the launch traced here: 31.8 us
  Pallas kernels  26.4 us (82%)
  local copies, waits for them, and re-layouts  3.41 us (11%)
  between operations  1.96 us (6%)
    pallas_call x1, Pallas kernels, local(): pl.pallas_call(functools.partial(kernel, n_inst, n_aa, kv_heads), out_sha...  25.5 us
    unnamed x12, local copies, waits for them, and re-layouts  3.41 us
    pallas_call x1, Pallas kernels, local(): pl.pallas_call(finish, out_shape=(jax.ShapeDtypeStruct(attended.shape, bf...  0.94 us

commit v1 on v0

v1 whole, which is shorter than its diff:
```python
import functools
import math

import jax
import jax.numpy as jnp
from jax import lax
from jax.experimental import pallas as pl
from jax.experimental.pallas import tpu as pltpu
from jax.sharding import PartitionSpec as P

HEAD_DIM = 128
MOST = 2
LANES = 128
BLOCK = 256
NEG_LARGE = -1e30
MESH = pl.DeviceIdType.MESH


def kernel(
    n_inst, n_aa, kv_heads,
    table_ref, len_ref, page_ref, dest_ref, q_hbm, pool_hbm, fresh_hbm,
    out_ref,
    q_ref, pool_ref, fresh_ref,
    st_mov, st_rn, st_near, st_fwd, raw, raw_far, kv_mov, kv_rn, metas,
    run_max, run_sum, run_out, q_turned,
    s_load, s_all, r_rn, r_mov, r_raw, r_far, r_row, r_meta,
):
    b = lax.axis_index("ba")
    a = lax.axis_index("aa")
    share = n_aa // kv_heads
    mine, member = a // share, a % share
    half = n_inst // 2
    side = b // half
    base = side * half
    pos = b - base
    hub = half - 1 + side
    far_hub = half - side
    far_base = half - base
    is_hub = b == hub
    reach = (1 - side) * (half - 1 - pos) + side * pos
    near_count = half - 1
    far_count = half
    table = table_ref.shape[1]
    moves = page_ref.shape[1]
    page_rows = pool_ref.shape[1]
    fresh = fresh_ref.shape[0]
    queries = q_ref.shape[0]
    heads = q_ref.shape[1] // HEAD_DIM
    bits = (n_inst - 1).bit_length()

    def near(k):
        return base + lax.rem(pos + k + half, half)

    def flip(j):
        to = mine
        bit = 1
        while bit <= j:
            if j & bit:
                to = to + bit - 2 * bit * (mine // bit % 2)
            bit *= 2
        return to

    def at_head(j):
        return flip(j) * share + member

    def peer(k):
        return mine * share + lax.rem(member + k, share)

    pool_load = pltpu.make_async_copy(pool_hbm, pool_ref, s_load.at[0])
    pool_load.start()
    q_load = pltpu.make_async_copy(q_hbm, q_ref, s_load.at[1])
    q_load.start()
    fresh_load = pltpu.make_async_copy(fresh_hbm, fresh_ref, s_load.at[2])
    fresh_load.start()

    barrier = pltpu.get_barrier_semaphore()
    partners = [(b, at_head(j)) for j in range(1, kv_heads)]
    partners += [(b, peer(k)) for k in range(1, share)]
    partners += [(near(k), a) for k in range(1, half)]
    partners += [(far_base + f, a) for f in range(half)]
    for ba, aa in partners:
        pl.semaphore_signal(barrier, inc=1, device_id={"ba": ba, "aa": aa}, device_id_type=MESH)

    def columns_of(h):
        return slice(h * HEAD_DIM, (h + 1) * HEAD_DIM)

    code = len_ref[0, 0]
    for i in range(moves):
        code = code * (1 << bits) + dest_ref[0, i]
    metas[0, 0, 0] = jnp.full((1, LANES), code, jnp.int32)

    pool_load.wait()
    for h in range(kv_heads):
        for i in range(moves):
            for w in range(2):
                st_mov[h, i, w] = pool_ref[page_ref[0, i], :, w, columns_of(h)]

    def remote(src, dst, ss, rs, ba, aa):
        return pltpu.make_async_remote_copy(
            src_ref=src, dst_ref=dst, send_sem=ss, recv_sem=rs,
            device_id={"ba": ba, "aa": aa}, device_id_type=MESH,
        )

    sent, hub_sent = [], []

    def start(src, dst, rs, ba, aa, kept=sent, spot=None):
        c = remote(src, dst, s_all.at[len(sent) + len(hub_sent)], rs, ba, aa)
        c.start()
        kept.append((spot or src, len(sent) + len(hub_sent)))

    def arrived(slot, rs):
        remote(slot, slot, s_all.at[0], rs, b, a).wait_recv()

    def shifted(row, count):
        return lax.shift_right_logical(row, jnp.full(row.shape, count, jnp.int32))

    def dests_of(row):
        low = jnp.full(row.shape, (1 << bits) - 1, jnp.int32)
        return [lax.bitwise_and(shifted(row, bits * (moves - 1 - i)), low) for i in range(moves)]

    def picks(row, target):
        seen = jnp.zeros((1, LANES), jnp.int32)
        chosen = [[] for _ in range(MOST)]
        for dest in dests_of(row):
            hit = (dest == target).astype(jnp.int32)
            for m in range(MOST):
                chosen[m].append(hit * (seen == m).astype(jnp.int32))
            seen = seen + hit
        return chosen

    def select(pages, row, target, into):
        chosen = picks(row, target)
        for m in range(MOST):
            masks = [jnp.broadcast_to(c.astype(jnp.float32), (page_rows, LANES)).astype(jnp.bfloat16) for c in chosen[m]]
            for w in range(2):
                total = pages[0, w] * masks[0]
                for i in range(1, moves):
                    total = total + pages[i, w] * masks[i]
                into[w, m * page_rows:(m + 1) * page_rows, :] = total

    def to_peers(buf, sems, *at):
        for k in range(1, share):
            lead, tail = at[:-1], at[-1:]
            there = (*lead, share - k, *tail)
            here = (*lead, 0, *tail)
            start(buf.at[here], buf.at[there], sems.at[there], b, peer(k))

    def send_moved(j):
        own = st_mov.at[mine] if j == 0 else raw.at[j]
        if j:
            arrived(raw.at[j], r_raw.at[j])
        start(own, raw_far.at[reach, j], r_far.at[reach, j], far_hub, a)
        if half > 1:
            if j:
                arrived(metas.at[0, 0, j], r_row.at[j])
            row = metas[0, 0, j]
            for k in range(1, half):
                select(own, row, near(k), st_near.at[k - 1, j])
                start(st_near.at[k - 1, j], kv_mov.at[k - 1, 0, j], r_mov.at[k - 1, 0, j], near(k), a)
        elif j:
            arrived(metas.at[0, 0, j], r_row.at[j])

    pl.semaphore_wait(barrier, len(partners))

    start(st_mov.at[mine], raw_far.at[reach, 0], r_far.at[reach, 0], far_hub, a)
    for j in range(1, kv_heads):
        start(metas.at[0, 0, 0], metas.at[0, 0, j], r_row.at[j], b, at_head(j))
    for j in range(1, kv_heads):
        start(st_mov.at[flip(j)], raw.at[j], r_raw.at[j], b, at_head(j))
    for k in range(1, half):
        select(st_mov.at[mine], metas[0, 0, 0], near(k), st_near.at[k - 1, 0])
        start(st_near.at[k - 1, 0], kv_mov.at[k - 1, 0, 0], r_mov.at[k - 1, 0, 0], near(k), a)

    fresh_load.wait()
    for h in range(kv_heads):
        for w in range(2):
            st_rn[h, w, 0:fresh, :] = fresh_ref[:, w, columns_of(h)]
            for i in range(table):
                st_rn[h, w, fresh + i * page_rows:fresh + (i + 1) * page_rows, :] = pool_ref[table_ref[0, i], :, w, columns_of(h)]
    for k in range(1, share):
        start(st_rn.at[mine], kv_rn.at[share - k, 0], r_rn.at[share - k, 0], b, peer(k))
    for j in range(1, kv_heads):
        start(st_rn.at[flip(j)], kv_rn.at[0, j], r_rn.at[0, j], b, at_head(j))

    q_load.wait()
    for h in range(heads):
        q_turned[:, h * queries:(h + 1) * queries] = q_ref[:, h * HEAD_DIM:(h + 1) * HEAD_DIM].T

    scale = math.log2(math.e) / math.sqrt(HEAD_DIM)

    def attend(keys, values, bias, first):
        turned = values.T
        copies = BLOCK // bias.shape[1]
        wide = jnp.concatenate([bias] * copies, axis=1) if copies > 1 else bias
        for start_at in range(0, heads * queries, BLOCK):
            block = slice(start_at, start_at + BLOCK)
            s = jnp.dot(keys, q_turned[:, block], preferred_element_type=jnp.float32)
            s = s * scale + wide
            top = jnp.max(s, axis=0, keepdims=True)
            if not first:
                old = run_max[:, block]
                top = jnp.maximum(old, top)
            w = jnp.exp2(s - top)
            total = jnp.sum(w, axis=0, keepdims=True)
            high = w.astype(jnp.bfloat16)
            low = (w - high.astype(jnp.float32)).astype(jnp.bfloat16)
            out = jnp.dot(turned, high, preferred_element_type=jnp.float32)
            out = out + jnp.dot(turned, low, preferred_element_type=jnp.float32)
            if not first:
                shrink = jnp.exp2(old - top)
                total = total + run_sum[:, block] * shrink
                out = out + run_out[:, block] * shrink
            run_max[:, block] = top
            run_sum[:, block] = total
            run_out[:, block] = out

    def rows_of(kk, j):
        return st_rn.at[mine] if kk == 0 and j == 0 else kv_rn.at[kk, j]

    place = lax.broadcasted_iota(jnp.int32, (table * page_rows, LANES), 0)

    def attend_resident(spots, first=False):
        biases = []
        for kk, j in spots:
            live = shifted(metas[0, kk, j], bits * moves)
            biases.append(jnp.where(place < live, 0.0, NEG_LARGE))
        attend(
            jnp.concatenate([rows_of(kk, j)[0, fresh:] for kk, j in spots], axis=0),
            jnp.concatenate([rows_of(kk, j)[1, fresh:] for kk, j in spots], axis=0),
            jnp.concatenate(biases, axis=0), first,
        )

    def attend_fresh():
        spots = [(kk, j) for j in range(kv_heads) for kk in range(share)]
        line = lax.broadcasted_iota(jnp.int32, (fresh, queries), 0)
        column = lax.broadcasted_iota(jnp.int32, (fresh, queries), 1)
        biases = []
        for kk, j in spots:
            owner = flip(j) * share + lax.rem(member + kk, share)
            biases.append(jnp.where(line + owner * fresh <= column, 0.0, NEG_LARGE))
        attend(
            jnp.concatenate([rows_of(kk, j)[0, :fresh] for kk, j in spots], axis=0),
            jnp.concatenate([rows_of(kk, j)[1, :fresh] for kk, j in spots], axis=0),
            jnp.concatenate(biases, axis=0), False,
        )

    def attend_moved(spots):
        biases = []
        for i, kk, j in spots:
            chosen = picks(metas[1 + i, kk, j], b)
            for m in range(MOST):
                taken = chosen[m][0]
                for c in chosen[m][1:]:
                    taken = taken + c
                biases.append(jnp.broadcast_to(jnp.where(taken > 0, 0.0, NEG_LARGE), (page_rows, LANES)))
        attend(
            jnp.concatenate([kv_mov[i, kk, j, 0] for i, kk, j in spots], axis=0),
            jnp.concatenate([kv_mov[i, kk, j, 1] for i, kk, j in spots], axis=0),
            jnp.concatenate(biases, axis=0), False,
        )

    def relay_rows(j):
        arrived(kv_rn.at[0, j], r_rn.at[0, j])
        to_peers(kv_rn, r_rn, j)

    def peers_rows(j):
        for kk in range(1, share):
            arrived(kv_rn.at[kk, j], r_rn.at[kk, j])

    def relay_near(k, j):
        arrived(kv_mov.at[k, 0, j], r_mov.at[k, 0, j])
        to_peers(kv_mov, r_mov, k, j)

    def relay_far(e, j):
        i = near_count + e

        @pl.when(is_hub)
        def _():
            arrived(raw_far.at[e, j], r_far.at[e, j])
            row = metas[1 + i, 0, j]
            for k in range(1, half):
                select(raw_far.at[e, j], row, near(k), st_fwd.at[e, j, k - 1])
                start(st_fwd.at[e, j, k - 1], kv_mov.at[i, 0, j], r_mov.at[i, 0, j], near(k), a, hub_sent, (st_fwd, e, j, k - 1))
            select(raw_far.at[e, j], row, b, kv_mov.at[i, 0, j])

        if half > 1:
            @pl.when(jnp.logical_not(is_hub))
            def _():
                arrived(kv_mov.at[i, 0, j], r_mov.at[i, 0, j])

        to_peers(kv_mov, r_mov, i, j)

    def peers_moved(i, j):
        for kk in range(1, share):
            arrived(kv_mov.at[i, kk, j], r_mov.at[i, kk, j])

    def send_metas():
        for k in range(1, share):
            start(metas.at[0, 0], metas.at[0, share - k], r_meta.at[0, share - k], b, peer(k))
        start(metas.at[0, 0], metas.at[1 + near_count + reach, 0], r_meta.at[1 + near_count + reach, 0], far_hub, a)
        for k in range(1, half):
            start(metas.at[0, 0], metas.at[k, 0], r_meta.at[k, 0], near(k), a)

    def near_metas():
        for k in range(1, half):
            arrived(metas.at[k, 0], r_meta.at[k, 0])
            for p in range(1, share):
                start(metas.at[k, 0], metas.at[k, share - p], r_meta.at[k, share - p], b, peer(p))

    def far_metas(e):
        g = 1 + near_count + e
        arrived(metas.at[g, 0], r_meta.at[g, 0])
        if half > 1:
            @pl.when(is_hub)
            def _():
                for k in range(1, half):
                    start(metas.at[g, 0], metas.at[g, 0], r_meta.at[g, 0], near(k), a, hub_sent, (metas, g, 0))
        for p in range(1, share):
            start(metas.at[g, 0], metas.at[g, share - p], r_meta.at[g, share - p], b, peer(p))

    def peers_metas(g):
        for kk in range(1, share):
            arrived(metas.at[g, kk], r_meta.at[g, kk])

    members = range(share)
    for j in range(1, kv_heads):
        send_moved(j)
        if j == 1:
            attend_resident([(0, 0)], True)
    send_metas()
    for k in range(near_count):
        relay_near(k, 0)
    near_metas()
    for e in range(far_count):
        far_metas(e)
    for e in range(far_count):
        relay_far(e, 0)
    peers_metas(0)
    for j in range(1, kv_heads):
        peers_rows(0) if j == 1 else None
        if j == 1:
            attend_resident([(kk, 0) for kk in range(1, share)])
        relay_rows(j)
        for k in range(near_count):
            relay_near(k, j)
    for g in range(1, 1 + near_count + far_count):
        peers_metas(g)
    for j in range(1, kv_heads):
        for e in range(far_count):
            relay_far(e, j)
        peers_rows(j)
        attend_resident([(kk, j) for kk in members])
        for i in range(near_count):
            peers_moved(i, j - 1)
            attend_moved([(i, kk, j - 1) for kk in members])
        if j == kv_heads - 1:
            attend_fresh()
            for i in range(near_count):
                peers_moved(i, j)
                attend_moved([(i, kk, j) for kk in members])
        for e in range(far_count):
            peers_moved(near_count + e, j - 1)
        attend_moved([(near_count + e, kk, j - 1) for e in range(far_count) for kk in members])
    j = kv_heads - 1
    for e in range(far_count):
        peers_moved(near_count + e, j)
    attend_moved([(near_count + e, kk, j) for e in range(far_count) for kk in members])

    def turn(h):
        part = slice(h * queries, (h + 1) * queries)
        return (run_out[:, part] / run_sum[:, part]).T

    for h in range(heads):
        out_ref[:, h * HEAD_DIM:(h + 1) * HEAD_DIM] = turn(h).astype(out_ref.dtype)
    def left(src, n):
        remote(src, src, s_all.at[n], s_all.at[n], b, a).wait_send()

    for src, n in sent:
        left(src, n)
    if hub_sent:
        @pl.when(is_hub)
        def _():
            for spot, n in hub_sent:
                left(spot[0].at[spot[1:]], n)


def finish(append_ref, rows_ref, pool_ref, fresh_ref, out_ref, updated_ref):
    out_ref[...] = rows_ref[...]
    updated_ref[...] = pool_ref[...]
    updated_ref[append_ref[0, 0], 0:fresh_ref.shape[0]] = fresh_ref[...]


def local(n_inst, n_aa, queries, new_kv, pool, page_table, ctx_len, move_page, move_dest, append_page):
    pool_pages = pool[0]
    pages, page_rows, _, width = pool_pages.shape
    kv_heads = width // HEAD_DIM
    share = n_aa // kv_heads
    fresh_rows = new_kv[0]
    fresh_count = fresh_rows.shape[0]
    query_count, q_width = queries.shape[1:]
    heads = q_width // HEAD_DIM
    table = page_table.shape[1]
    moves = move_page.shape[1]
    half = n_inst // 2
    near, far = half - 1, half
    groups = 1 + near + far
    bf, f32 = jnp.bfloat16, jnp.float32
    dma = pltpu.SemaphoreType.DMA
    page = (2, page_rows, HEAD_DIM)
    slots = (2, MOST * page_rows, HEAD_DIM)
    rows = (2, fresh_count + table * page_rows, HEAD_DIM)
    attended = pl.pallas_call(
        functools.partial(kernel, n_inst, n_aa, kv_heads),
        out_shape=jax.ShapeDtypeStruct((query_count, q_width), bf),
        in_specs=[pl.BlockSpec(memory_space=pltpu.SMEM)] * 4 + [pl.BlockSpec(memory_space=pltpu.HBM)] * 3,
        out_specs=pl.BlockSpec(memory_space=pltpu.VMEM),
        scratch_shapes=[
            pltpu.VMEM((query_count, q_width), bf),
            pltpu.VMEM(pool_pages.shape, bf),
            pltpu.VMEM(fresh_rows.shape, bf),
            pltpu.VMEM((kv_heads, moves, *page), bf),
            pltpu.VMEM((kv_heads, *rows), bf),
            pltpu.VMEM((max(near, 1), kv_heads, *slots), bf),
            pltpu.VMEM((far, kv_heads, max(near, 1), *slots), bf),
            pltpu.VMEM((kv_heads, moves, *page), bf),
            pltpu.VMEM((far, kv_heads, moves, *page), bf),
            pltpu.VMEM((near + far, share, kv_heads, *slots), bf),
            pltpu.VMEM((share, kv_heads, *rows), bf),
            pltpu.VMEM((groups, share, kv_heads, 1, LANES), jnp.int32),
            pltpu.VMEM((1, heads * query_count), f32),
            pltpu.VMEM((1, heads * query_count), f32),
            pltpu.VMEM((HEAD_DIM, heads * query_count), f32),
            pltpu.VMEM((HEAD_DIM, heads * query_count), bf),
            dma((3,)), dma((400,)),
            dma((share, kv_heads)), dma((near + far, share, kv_heads)),
            dma((kv_heads,)), dma((far, kv_heads)), dma((kv_heads,)), dma((groups, share)),
        ],
        compiler_params=pltpu.CompilerParams(collective_id=0, has_side_effects=True, vmem_limit_bytes=48 * 2**20),
        name="paged_attention",
    )(page_table, ctx_len, move_page, move_dest, queries[0], pool_pages, fresh_rows)
    attended, updated = pl.pallas_call(
        finish,
        out_shape=(
            jax.ShapeDtypeStruct(attended.shape, bf),
            jax.ShapeDtypeStruct(pool_pages.shape, bf),
        ),
        in_specs=[pl.BlockSpec(memory_space=pltpu.SMEM)] + [pl.BlockSpec(memory_space=pltpu.VMEM)] * 3,
        out_specs=(pl.BlockSpec(memory_space=pltpu.VMEM),) * 2,
        compiler_params=pltpu.CompilerParams(vmem_limit_bytes=12 * 2**20),
        name="finish",
    )(append_page, attended, pool_pages, fresh_rows)
    return (attended[None], updated[None])


def solution(mesh):
    return jax.shard_map(
        functools.partial(local, mesh.shape["ba"], mesh.shape["aa"]),
        mesh=mesh,
        in_specs=(
            P("ba", None, "aa"),
            P("ba", "aa", None, None),
            P("ba", "aa", None, None, None),
            P("ba", "aa"),
            P("ba", "aa"),
            P("ba", "aa"),
            P("ba", "aa"),
            P("ba", "aa"),
        ),
        out_specs=(P("ba", None, "aa"), P("ba", "aa", None, None, None)),
        check_vma=False,
    )
```

time: 32.1 us -> 41 us (1.28)
  Pallas kernels: 26.4 us -> 35 us
    pallas_call x1, Pallas kernels: 25.5 us -> 34 us  [local(): pl.pallas_call(functools.partial(kernel, n_inst, n_aa, kv_heads), out_sha...]
where the time goes in v1:
time: 41 us; the launch traced here: 40.3 us
  Pallas kernels  35 us (85%)
  local copies, waits for them, and re-layouts  3.41 us (8%)
  between operations  1.96 us (5%)
    pallas_call x1, Pallas kernels, local(): pl.pallas_call(functools.partial(kernel, n_inst, n_aa, kv_heads), out_sha...  34 us
    unnamed x12, local copies, waits for them, and re-layouts  3.41 us
    pallas_call x1, Pallas kernels, local(): pl.pallas_call(finish, out_shape=(jax.ShapeDtypeStruct(attended.shape, bf...  0.94 us

profile of v1, /device:TPU:0, one launch (start us, length us, event | category | flops | bytes accessed | tf_op | source)
XLA Modules:
  0.0 40.3 jit_solution(12709950412961622836)
XLA Ops:
  1.9 0.0 copy-start.3
  1.9 0.0 copy-start.4
  1.9 0.0 copy-start.5
  2.0 0.6 %copy-done.3 = s32[1,4]{1,0:T(1,128)S(1)} copy-done((s32[1,4]{1,0:T(1,128)S(1)}, s32[1,4]{1,0:T(1,128)}, u32[]{:S(2)}) %copy-start.3) | copy-done | bytes 40
  2.6 0.0 copy-done.4
  2.6 0.0 copy-done.5
  2.6 0.0 copy-start
  2.6 1.0 %copy-done = bf16[1,8,32,2,512]{4,3,2,1,0:T(2,128)(2,1)S(1)} copy-done((bf16[1,8,32,2,512]{4,3,2,1,0:T(2,128)(2,1)S(1)}, bf16[1,8,32,2,512]{4,3,2,1,0:T(2,128)(2,1)}, u32[]{:S(2)}) %copy-start) | copy-done | bytes 524312
  3.7 0.0 copy-start.1
  3.7 0.9 %copy-done.1 = bf16[1,128,1024]{2,1,0:T(8,128)(2,1)S(1)} copy-done((bf16[1,128,1024]{2,1,0:T(8,128)(2,1)S(1)}, bf16[1,128,1024]{2,1,0:T(8,128)(2,1)}, u32[]{:S(2)}) %copy-start.1) | copy-done | bytes 262168
  4.6 0.0 copy-start.2
  4.6 0.8 %copy-done.2 = bf16[1,16,2,512]{3,2,1,0:T(2,128)(2,1)S(1)} copy-done((bf16[1,16,2,512]{3,2,1,0:T(2,128)(2,1)S(1)}, bf16[1,16,2,512]{3,2,1,0:T(2,128)(2,1)}, u32[]{:S(2)}) %copy-start.2) | copy-done | bytes 32792
  5.4 34.0 %paged_attention.1.rows_ref = bf16[128,1024]{1,0:T(8,128)(2,1)S(1)} custom-call(s32[1,4]{1,0:T(1,128)S(1)} %copy-done.3, s32[1,1]{1,0:T(1,128)S(6)} %copy.10.len_ref, s32[1,3]{1,0:T(1,128)S(1)} %copy-done.4, s32[1,3]{1,0:T(1,128)S(1)} %copy-done.5, bf16[128,1024]{1,0:T(8,128)(2,1)S(1)} %bitcast.7, bf16[8,32,2,512]{3,2,1,0:T(2,128)(2,1)S(1)} %bitcast.5, ...), custom_call_target="tpu_custom_call" | custom-call | tf_op jit(solution)/shard_map/paged_attention/pallas_call | solution.py:412
  39.4 0.9 %finish.1 = (bf16[128,1024]{1,0:T(8,128)(2,1)}, bf16[8,32,2,512]{3,2,1,0:T(2,128)(2,1)}) custom-call(s32[1,1]{1,0:T(1,128)S(6)} %copy.11.append_ref, bf16[128,1024]{1,0:T(8,128)(2,1)S(1)} %paged_attention.1.rows_ref, bf16[8,32,2,512]{3,2,1,0:T(2,128)(2,1)S(1)} %bitcast.6, bf16[16,2,512]{2,1,0:T(2,128)(2,1)S(1)} %bitcast.9), custom_call_target="tpu_custom_call" | custom-call | tf_op jit(solution)/shard_map/finish/pallas_call | solution.py:441
Async XLA Ops:
  1.9 0.7 %copy-start.3 = (s32[1,4]{1,0:T(1,128)S(1)}, s32[1,4]{1,0:T(1,128)}, u32[]{:S(2)}) copy-start(s32[1,4]{1,0:T(1,128)} %table_ref.1) | copy-start | bytes 52
  1.9 0.7 %copy-start.4 = (s32[1,3]{1,0:T(1,128)S(1)}, s32[1,3]{1,0:T(1,128)}, u32[]{:S(2)}) copy-start(s32[1,3]{1,0:T(1,128)} %page_ref.1) | copy-start | bytes 40
  1.9 0.7 %copy-start.5 = (s32[1,3]{1,0:T(1,128)S(1)}, s32[1,3]{1,0:T(1,128)}, u32[]{:S(2)}) copy-start(s32[1,3]{1,0:T(1,128)} %dest_ref.1) | copy-start | bytes 40
  2.6 1.0 %copy-start = (bf16[1,8,32,2,512]{4,3,2,1,0:T(2,128)(2,1)S(1)}, bf16[1,8,32,2,512]{4,3,2,1,0:T(2,128)(2,1)}, u32[]{:S(2)}) copy-start(bf16[1,8,32,2,512]{4,3,2,1,0:T(2,128)(2,1)} %param.10) | copy-start | bytes 1572868
  3.7 0.9 %copy-start.1 = (bf16[1,128,1024]{2,1,0:T(8,128)(2,1)S(1)}, bf16[1,128,1024]{2,1,0:T(8,128)(2,1)}, u32[]{:S(2)}) copy-start(bf16[1,128,1024]{2,1,0:T(8,128)(2,1)} %param.8) | copy-start | bytes 786436
  4.6 0.8 %copy-start.2 = (bf16[1,16,2,512]{3,2,1,0:T(2,128)(2,1)S(1)}, bf16[1,16,2,512]{3,2,1,0:T(2,128)(2,1)}, u32[]{:S(2)}) copy-start(bf16[1,16,2,512]{3,2,1,0:T(2,128)(2,1)} %param.9) | copy-start | bytes 98308

commit v2 on v1

v2 whole, which is shorter than its diff:
```python
import functools
import math

import jax
import jax.numpy as jnp
from jax import lax
from jax.experimental import pallas as pl
from jax.experimental.pallas import tpu as pltpu
from jax.sharding import PartitionSpec as P

HEAD_DIM = 128
MOST = 2
LANES = 128
BLOCK = 256
NEG_LARGE = -1e30
MESH = pl.DeviceIdType.MESH


def kernel(
    n_inst, n_aa, kv_heads,
    table_ref, len_ref, page_ref, dest_ref, q_hbm, pool_hbm, fresh_hbm,
    out_ref,
    q_ref, pool_ref, fresh_ref,
    ext, st_rn, st_out, passed, kv_mov, kv_rn, metas,
    run_max, run_sum, run_out, q_turned,
    s_load, s_all, r_rn, r_mov, r_peer, r_pass, r_row, r_meta, s_wide,
):
    b = lax.axis_index("ba")
    a = lax.axis_index("aa")
    share = n_aa // kv_heads
    mine, member = a // share, a % share
    half = n_inst // 2
    side = b // half
    base = side * half
    pos = b - base
    hub = half - 1 + side
    far_hub = half - side
    is_hub = b == hub
    reach = (1 - side) * (half - 1 - pos) + side * pos
    near_count = half - 1
    table = table_ref.shape[1]
    moves = page_ref.shape[1]
    page_rows = pool_ref.shape[1]
    fresh = fresh_ref.shape[0]
    queries = q_ref.shape[0]
    heads = q_ref.shape[1] // HEAD_DIM
    bits = (n_inst - 1).bit_length()
    shared = half == 2 and MOST == 2 and moves < 2 * MOST

    def near(k):
        return base + lax.rem(pos + k + half, half)

    def far(t):
        return far_hub + (1 - 2 * side) * t

    def flip(j):
        to = mine
        bit = 1
        while bit <= j:
            if j & bit:
                to = to + bit - 2 * bit * (mine // bit % 2)
            bit *= 2
        return to

    heads_at = [flip(j) for j in range(kv_heads)]
    device_at = [h * share + member for h in heads_at]
    peers = [mine * share + lax.rem(member + k, share) for k in range(share)]

    pool_load = pltpu.make_async_copy(pool_hbm, pool_ref, s_load.at[0])
    pool_load.start()
    q_load = pltpu.make_async_copy(q_hbm, q_ref, s_load.at[1])
    fresh_load = pltpu.make_async_copy(fresh_hbm, fresh_ref, s_load.at[2])
    fresh_load.start()
    q_load.start()

    barrier = pltpu.get_barrier_semaphore()
    partners = [(b, device_at[j]) for j in range(1, kv_heads)]
    partners += [(b, peers[k]) for k in range(1, share)]
    partners += [(near(k), to) for k in range(1, half) for to in device_at]
    partners += [(far(t), a) for t in range(half)]
    for ba, aa in partners:
        pl.semaphore_signal(barrier, inc=1, device_id={"ba": ba, "aa": aa}, device_id_type=MESH)

    def columns_of(h):
        return slice(h * HEAD_DIM, (h + 1) * HEAD_DIM)

    code = len_ref[0, 0]
    for i in range(moves):
        code = code * (1 << bits) + dest_ref[0, i]
    metas[0, 0, 0] = jnp.full((1, LANES), code, jnp.int32)

    def chosen_for(target):
        seen = jnp.int32(0)
        picked = [jnp.int32(0) for _ in range(MOST)]
        for i in range(moves):
            hit = (dest_ref[0, i] == target).astype(jnp.int32)
            for m in range(MOST):
                picked[m] = picked[m] + hit * (seen == m).astype(jnp.int32) * i
            seen = seen + hit
        return picked, seen

    outs = [(0, t, m) for m in reversed(range(1, MOST)) for t in range(half) if not (shared and t)]
    first_cut = len(outs)
    outs += [(0, t, 0) for t in reversed(range(half))]
    second_cut = len(outs)
    outs += [(1, k, m) for k in range(1, half) for m in range(MOST)]
    cuts = [(0, first_cut), (first_cut, second_cut)]
    out_count = st_out.shape[0] // kv_heads

    pool_load.wait()
    for i in range(moves):
        for h in range(kv_heads):
            for w in range(2):
                ext[i, h, w] = pool_ref[page_ref[0, i], :, w, columns_of(h)]
    picked_far = [chosen_for(far(t)) for t in range(half)]
    picked_near = [chosen_for(near(k)) for k in range(half)]
    for n, (kind, t, m) in enumerate(outs):
        index = (picked_near if kind else picked_far)[t][0][m]
        if shared and not kind and m == 1:
            index = jnp.where(picked_far[0][1] > 1, index, picked_far[1][0][1])
        for h in range(kv_heads):
            st_out[h * out_count + n] = ext[index, h]

    def remote(src, dst, ss, rs, ba, aa):
        return pltpu.make_async_remote_copy(
            src_ref=src, dst_ref=dst, send_sem=ss, recv_sem=rs,
            device_id={"ba": ba, "aa": aa}, device_id_type=MESH,
        )

    groups = metas.shape[0]
    wide = []
    pages = st_out.shape[0]
    kinds = {
        "page": (pages, lambda r: st_out.at[0:r]),
        "hub": (pages, lambda r: st_out.at[0:r]),
        "leaf": (pages, lambda r: st_out.at[0:r]),
        "pair": (pages // MOST, lambda r: st_out.at[0:r * MOST]),
        "rows": (kv_heads, lambda r: st_rn.at[0:r]),
        "row": (kv_heads, lambda r: metas.at[0, 0, 0:r]),
        "block": (groups, lambda r: metas.at[0:r, 0]),
    }
    names = list(kinds)
    counts = {name: 0 for name in names}
    per_kind = s_all.shape[1]

    def start(kind, src, dst, rs, ba, aa):
        n = counts[kind] // kinds[kind][0]
        assert n < per_kind
        counts[kind] += 1
        remote(src, dst, s_all.at[names.index(kind), n], rs, ba, aa).start()

    def all_left(kind):
        size, piece = kinds[kind]
        for n in range(0, counts[kind], size):
            ref = piece(min(size, counts[kind] - n))
            remote(ref, ref, s_all.at[names.index(kind), n // size], s_load.at[0], b, a).wait_send()

    def arrived(slot, rs):
        remote(slot, slot, s_load.at[0], rs, b, a).wait_recv()

    def shifted(row, count):
        return lax.shift_right_logical(row, jnp.full(row.shape, count, jnp.int32))

    def taken(row, target):
        low = jnp.full(row.shape, (1 << bits) - 1, jnp.int32)
        count = jnp.zeros(row.shape, jnp.int32)
        for i in range(moves):
            dest = lax.bitwise_and(shifted(row, bits * (moves - 1 - i)), low)
            count = count + (dest == target).astype(jnp.int32)
        return count

    fresh_load.wait()
    for h in range(kv_heads):
        for w in range(2):
            st_rn[h, w, 0:fresh, :] = fresh_ref[:, w, columns_of(h)]
            for i in range(table):
                st_rn[h, w, fresh + i * page_rows:fresh + (i + 1) * page_rows, :] = pool_ref[table_ref[0, i], :, w, columns_of(h)]
    pl.semaphore_wait(barrier, len(partners))

    def source(j, lo, hi):
        return st_out.at[pl.ds(mine * out_count + lo, hi - lo)] if j == 0 else passed.at[j, lo:hi]

    def send_on(j, part):
        lo, hi = cuts[part]
        if j:
            arrived(passed.at[j, lo:hi], r_pass.at[j, part])
        i = near_count + reach
        for n in range(lo, hi):
            _, t, m = outs[n]
            start("page", source(j, n, n + 1), kv_mov.at[i, 0, j, m:m + 1], r_mov.at[i, j, m], far(t), a)

    def send_near(j):
        for k in range(1, half):
            n = second_cut + (k - 1) * MOST
            start("pair", st_out.at[pl.ds(heads_at[j] * out_count + n, MOST)], kv_mov.at[k - 1, 0, j], r_mov.at[k - 1, j, 0], near(k), device_at[j])

    def send_plane(j, part):
        lo, hi = cuts[part]
        kind = {1: "page", 2: "pair"}
        src, dst = st_out.at[pl.ds(heads_at[j] * out_count + lo, hi - lo)], passed.at[j, lo:hi]
        if hi - lo in kind:
            start(kind[hi - lo], src, dst, r_pass.at[j, part], b, device_at[j])
        else:
            wide.append((src, j, part))
            remote(src, dst, s_wide.at[j, part], r_pass.at[j, part], b, device_at[j]).start()

    send_on(0, 0)
    for j in range(1, kv_heads):
        start("row", metas.at[0, 0, 0], metas.at[0, 0, j], r_row.at[0], b, device_at[j])
    for j in range(1, kv_heads):
        send_plane(j, 0)
    send_near(0)
    send_on(0, 1)
    for j in range(1, kv_heads):
        send_plane(j, 1)
    for k in range(1, share):
        start("rows", st_rn.at[mine], kv_rn.at[share - k, 0], r_rn.at[share - k, 0], b, peers[k])

    q_load.wait()
    for h in range(heads):
        q_turned[:, h * queries:(h + 1) * queries] = q_ref[:, h * HEAD_DIM:(h + 1) * HEAD_DIM].T

    scale = math.log2(math.e) / math.sqrt(HEAD_DIM)

    def attend(keys, values, bias, first):
        turned = values.T
        copies = BLOCK // bias.shape[1]
        wide = jnp.concatenate([bias] * copies, axis=1) if copies > 1 else bias
        for start_at in range(0, heads * queries, BLOCK):
            block = slice(start_at, start_at + BLOCK)
            s = jnp.dot(keys, q_turned[:, block], preferred_element_type=jnp.float32)
            s = s * scale + wide
            top = jnp.max(s, axis=0, keepdims=True)
            if not first:
                old = run_max[:, block]
                top = jnp.maximum(old, top)
            w = jnp.exp2(s - top)
            total = jnp.sum(w, axis=0, keepdims=True)
            high = w.astype(jnp.bfloat16)
            low = (w - high.astype(jnp.float32)).astype(jnp.bfloat16)
            out = jnp.dot(turned, high, preferred_element_type=jnp.float32)
            out = out + jnp.dot(turned, low, preferred_element_type=jnp.float32)
            if not first:
                shrink = jnp.exp2(old - top)
                total = total + run_sum[:, block] * shrink
                out = out + run_out[:, block] * shrink
            run_max[:, block] = top
            run_sum[:, block] = total
            run_out[:, block] = out

    def rows_of(kk, j):
        return st_rn.at[mine] if kk == 0 and j == 0 else kv_rn.at[kk, j]

    place = lax.broadcasted_iota(jnp.int32, (table * page_rows, LANES), 0)

    def attend_resident(spots, first=False):
        biases = []
        for kk, j in spots:
            live = shifted(metas[0, kk, j], bits * moves)
            biases.append(jnp.where(place < live, 0.0, NEG_LARGE))
        attend(
            jnp.concatenate([rows_of(kk, j)[0, fresh:] for kk, j in spots], axis=0),
            jnp.concatenate([rows_of(kk, j)[1, fresh:] for kk, j in spots], axis=0),
            jnp.concatenate(biases, axis=0), first,
        )

    def attend_fresh():
        spots = [(kk, j) for j in range(kv_heads) for kk in range(share)]
        line = lax.broadcasted_iota(jnp.int32, (fresh, queries), 0)
        column = lax.broadcasted_iota(jnp.int32, (fresh, queries), 1)
        biases = []
        for kk, j in spots:
            owner = heads_at[j] * share + lax.rem(member + kk, share)
            biases.append(jnp.where(line + owner * fresh <= column, 0.0, NEG_LARGE))
        attend(
            jnp.concatenate([rows_of(kk, j)[0, :fresh] for kk, j in spots], axis=0),
            jnp.concatenate([rows_of(kk, j)[1, :fresh] for kk, j in spots], axis=0),
            jnp.concatenate(biases, axis=0), False,
        )

    def attend_moved(spots):
        biases = []
        for i, kk, j, m in spots:
            count = taken(metas[1 + i, kk, j], b)
            biases.append(jnp.broadcast_to(jnp.where(count > m, 0.0, NEG_LARGE), (page_rows, LANES)))
        attend(
            jnp.concatenate([kv_mov[i, kk, j, m, 0] for i, kk, j, m in spots], axis=0),
            jnp.concatenate([kv_mov[i, kk, j, m, 1] for i, kk, j, m in spots], axis=0),
            jnp.concatenate(biases, axis=0), False,
        )

    members = range(share)
    chips = range(kv_heads)
    slots = range(MOST)

    def relay_rows(j):
        arrived(kv_rn.at[0, j], r_rn.at[0, j])
        for k in range(1, share):
            start("rows", kv_rn.at[0, j], kv_rn.at[share - k, j], r_rn.at[share - k, j], b, peers[k])

    def peers_rows(j):
        for kk in range(1, share):
            arrived(kv_rn.at[kk, j], r_rn.at[kk, j])

    def relay_near(j):
        for k in range(near_count):
            arrived(kv_mov.at[k, 0, j], r_mov.at[k, j, 0])
            for p in range(1, share):
                start("pair", kv_mov.at[k, 0, j], kv_mov.at[k, share - p, j], r_peer.at[k, share - p - 1, j // 2], b, peers[p])

    def relay_far(e, j, m):
        i = near_count + e
        spot = kv_mov.at[i, 0, j, m]
        arrived(spot, r_mov.at[i, j, m])
        for p in range(1, share):
            start("page", spot, kv_mov.at[i, share - p, j, m], r_peer.at[i, share - p - 1, m], b, peers[p])

    def hub_relay(spots):
        @pl.when(is_hub)
        def _():
            for e, j in spots:
                i = near_count + e
                spot = kv_mov.at[i, 0, j, 1]
                arrived(spot, r_mov.at[i, j, 1])
                start("hub", spot, kv_mov.at[i, 0, j, 1], r_mov.at[i, j, 1], near(1), a)
                for p in range(1, share):
                    start("hub", spot, kv_mov.at[i, share - p, j, 1], r_peer.at[i, share - p - 1, 1], b, peers[p])

    def leaf_relay(spots):
        @pl.when(jnp.logical_not(is_hub))
        def _():
            for e, j in spots:
                i = near_count + e
                spot = kv_mov.at[i, 0, j, 1]
                arrived(spot, r_mov.at[i, j, 1])
                for p in range(1, share):
                    start("leaf", spot, kv_mov.at[i, share - p, j, 1], r_peer.at[i, share - p - 1, 1], b, peers[p])

    def send_metas():
        arrived(metas.at[0, 0, 1:kv_heads], r_row.at[0])
        block = metas.at[0, 0]
        for t in range(half):
            g = 1 + near_count + reach
            start("block", block, metas.at[g, 0], r_meta.at[g, 0], far(t), a)
        for k in range(1, half):
            start("block", block, metas.at[k, 0], r_meta.at[k, 0], near(k), a)
        for p in range(1, share):
            start("block", block, metas.at[0, share - p], r_meta.at[0, share - p], b, peers[p])

    def relay_metas():
        for g in range(1, groups):
            arrived(metas.at[g, 0], r_meta.at[g, 0])
            for p in range(1, share):
                start("block", metas.at[g, 0], metas.at[g, share - p], r_meta.at[1, share - p], b, peers[p])

    def peers_metas(lo, hi):
        for kk in range(1, share):
            arrived(metas.at[lo:hi, kk], r_meta.at[lo, kk])

    def do_resident(j):
        peers_rows(j)
        attend_resident([(kk, j) for kk in members])

    def do_near(part):
        js = list(chips)[2 * part:2 * part + 2]
        for k in range(near_count):
            for kk in range(1, share):
                arrived(kv_mov.at[k, kk, js[0]:js[-1] + 1], r_peer.at[k, kk - 1, part])
            attend_moved([(k, kk, j, m) for j in js for kk in members for m in slots])

    def do_far(e, m):
        i = near_count + e
        for kk in range(1, share):
            arrived(kv_mov.at[i, kk, :, m], r_peer.at[i, kk - 1, m])
        attend_moved([(i, kk, j, m) for j in chips for kk in members])

    late = [m for m in reversed(slots) if m == 0 or not shared]

    def relay_late(j):
        for e in range(half):
            for m in late:
                relay_far(e, j, m)

    attend_resident([(0, 0)], True)
    send_on(1, 0)
    send_on(2, 0)
    send_metas()
    peers_metas(0, 1)
    send_on(3, 0)
    send_on(1, 1)
    send_on(2, 1)
    for j in range(1, kv_heads):
        send_near(j)
    peers_rows(0)
    attend_resident([(kk, 0) for kk in range(1, share)])
    if shared:
        hub_relay([(0, 0), (1, 0), (0, 1)])
    send_on(3, 1)
    for j in range(1, kv_heads):
        start("rows", st_rn.at[heads_at[j]], kv_rn.at[0, j], r_rn.at[0, j], b, device_at[j])
    relay_metas()
    if shared:
        hub_relay([(0, 2), (0, 3), (1, 1)])
    relay_near(0)
    relay_late(0)
    if shared:
        hub_relay([(1, 2), (1, 3)])
    relay_near(1)
    peers_metas(1, groups)
    do_near(0)
    relay_rows(1)
    relay_rows(2)
    relay_near(2)
    relay_late(1)
    do_resident(1)
    relay_rows(3)
    relay_near(3)
    do_resident(2)
    relay_late(2)
    do_near(1)
    do_resident(3)
    relay_late(3)
    attend_fresh()
    if shared:
        leaf_relay([(e, j) for j in chips for e in range(half)])
        do_far(0, 1)
        do_far(1, 1)
    for m in late:
        for e in range(half):
            do_far(e, m)

    def turn(h):
        part = slice(h * queries, (h + 1) * queries)
        return (run_out[:, part] / run_sum[:, part]).T

    for h in range(heads):
        out_ref[:, h * HEAD_DIM:(h + 1) * HEAD_DIM] = turn(h).astype(out_ref.dtype)

    for name in names:
        if name not in ("hub", "leaf"):
            all_left(name)
    for src, j, part in wide:
        remote(src, src, s_wide.at[j, part], s_load.at[0], b, a).wait_send()
    if shared:
        @pl.when(is_hub)
        def _():
            all_left("hub")

        @pl.when(jnp.logical_not(is_hub))
        def _():
            all_left("leaf")


def finish(append_ref, rows_ref, pool_ref, fresh_ref, out_ref, updated_ref):
    out_ref[...] = rows_ref[...]
    updated_ref[...] = pool_ref[...]
    updated_ref[append_ref[0, 0], 0:fresh_ref.shape[0]] = fresh_ref[...]


def local(n_inst, n_aa, queries, new_kv, pool, page_table, ctx_len, move_page, move_dest, append_page):
    pool_pages = pool[0]
    pages, page_rows, _, width = pool_pages.shape
    kv_heads = width // HEAD_DIM
    share = n_aa // kv_heads
    fresh_rows = new_kv[0]
    fresh_count = fresh_rows.shape[0]
    query_count, q_width = queries.shape[1:]
    heads = q_width // HEAD_DIM
    table = page_table.shape[1]
    moves = move_page.shape[1]
    half = n_inst // 2
    near = half - 1
    groups = 1 + near + half
    out_count = (near + half) * MOST
    per_kind = 3 if share < 4 else 9
    bf, f32 = jnp.bfloat16, jnp.float32
    dma = pltpu.SemaphoreType.DMA
    page = (2, page_rows, HEAD_DIM)
    rows = (2, fresh_count + table * page_rows, HEAD_DIM)
    attended = pl.pallas_call(
        functools.partial(kernel, n_inst, n_aa, kv_heads),
        out_shape=pltpu.VMEM((query_count, q_width), bf),
        in_specs=[pl.BlockSpec(memory_space=pltpu.SMEM)] * 4 + [pl.BlockSpec(memory_space=pltpu.HBM)] * 3,
        out_specs=pl.BlockSpec(memory_space=pltpu.VMEM),
        scratch_shapes=[
            pltpu.VMEM((query_count, q_width), bf),
            pltpu.VMEM(pool_pages.shape, bf),
            pltpu.VMEM(fresh_rows.shape, bf),
            pltpu.VMEM((moves, kv_heads, *page), bf),
            pltpu.VMEM((kv_heads, *rows), bf),
            pltpu.VMEM((kv_heads * out_count, *page), bf),
            pltpu.VMEM((kv_heads, out_count, *page), bf),
            pltpu.VMEM((near + half, share, kv_heads, MOST, *page), bf),
            pltpu.VMEM((share, kv_heads, *rows), bf),
            pltpu.VMEM((groups, share, kv_heads, 1, LANES), jnp.int32),
            pltpu.VMEM((1, heads * query_count), f32),
            pltpu.VMEM((1, heads * query_count), f32),
            pltpu.VMEM((HEAD_DIM, heads * query_count), f32),
            pltpu.VMEM((HEAD_DIM, heads * query_count), bf),
            dma((3,)), dma((7, per_kind)),
            dma((share, kv_heads)), dma((near + half, kv_heads, MOST)), dma((near + half, share - 1, MOST)),
            dma((kv_heads, 2)), dma((1,)), dma((groups, share)), dma((kv_heads, 2) if half > 2 else (1, 1)),
        ],
        compiler_params=pltpu.CompilerParams(collective_id=0, has_side_effects=True, vmem_limit_bytes=60 * 2**20),
        name="paged_attention",
    )(page_table, ctx_len, move_page, move_dest, queries[0], pool_pages, fresh_rows)
    attended, updated = pl.pallas_call(
        finish,
        out_shape=(
            jax.ShapeDtypeStruct(attended.shape, bf),
            jax.ShapeDtypeStruct(pool_pages.shape, bf),
        ),
        in_specs=[pl.BlockSpec(memory_space=pltpu.SMEM)] + [pl.BlockSpec(memory_space=pltpu.VMEM)] * 3,
        out_specs=(pl.BlockSpec(memory_space=pltpu.VMEM),) * 2,
        compiler_params=pltpu.CompilerParams(vmem_limit_bytes=12 * 2**20),
        name="finish",
    )(append_page, attended, pool_pages, fresh_rows)
    return (attended[None], updated[None])


def solution(mesh):
    return jax.shard_map(
        functools.partial(local, mesh.shape["ba"], mesh.shape["aa"]),
        mesh=mesh,
        in_specs=(
            P("ba", None, "aa"),
            P("ba", "aa", None, None),
            P("ba", "aa", None, None, None),
            P("ba", "aa"),
            P("ba", "aa"),
            P("ba", "aa"),
            P("ba", "aa"),
            P("ba", "aa"),
        ),
        out_specs=(P("ba", None, "aa"), P("ba", "aa", None, None, None)),
        check_vma=False,
    )
```

time: 41 us -> 30.1 us (0.73); the launches traced: 40.3 us -> 29.9 us
  Pallas kernels: 35 us -> 27.9 us
  local copies, waits for them, and re-layouts: 3.41 us -> 0.01 us
    pallas_call x1, Pallas kernels: 34 us -> 27 us  [local(): pl.pallas_call(functools.partial(kernel, n_inst, n_aa, kv_heads), out_sha...]
    unnamed x12 -> x4, local copies, waits for them, and re-layouts: 3.41 us -> 0.01 us
where the time goes in v2:
time: 30.1 us; the launch traced here: 29.9 us
  Pallas kernels  27.9 us (93%)
  between operations  1.96 us (7%)
    pallas_call x1, Pallas kernels, local(): pl.pallas_call(functools.partial(kernel, n_inst, n_aa, kv_heads), out_sha...  27 us
    pallas_call x1, Pallas kernels, local(): pl.pallas_call(finish, out_shape=(jax.ShapeDtypeStruct(attended.shape, bf...  0.94 us

profile of v2, /device:TPU:0, one launch (start us, length us, event | category | flops | bytes accessed | tf_op | source)
XLA Modules:
  0.0 29.9 jit_solution(11988606240465356372)
XLA Ops:
  1.9 0.0 copy-start
  1.9 0.0 copy-start.1
  1.9 27.0 %paged_attention.1.rows_ref = bf16[128,1024]{1,0:T(8,128)(2,1)S(1)} custom-call(s32[1,4]{1,0:T(1,128)} %table_ref.1, s32[1,1]{1,0:T(1,128)S(6)} %copy.10.len_ref, s32[1,3]{1,0:T(1,128)} %page_ref.1, s32[1,3]{1,0:T(1,128)} %dest_ref.1, bf16[128,1024]{1,0:T(8,128)(2,1)} %bitcast.9, bf16[8,32,2,512]{3,2,1,0:T(2,128)(2,1)} %bitcast.5, bf16[16,2,512]{2,1,0:T(2,128)(2,1)} %bitcast.7), custom_call_target="tpu_custom_call" | custom-call | tf_op jit(solution)/shard_map/paged_attention/pallas_call | solution.py:480
  28.9 0.0 copy-done
  28.9 0.0 copy-done.1
  28.9 0.9 %finish.1 = (bf16[128,1024]{1,0:T(8,128)(2,1)}, bf16[8,32,2,512]{3,2,1,0:T(2,128)(2,1)}) custom-call(s32[1,1]{1,0:T(1,128)S(6)} %copy.11.append_ref, bf16[128,1024]{1,0:T(8,128)(2,1)S(1)} %paged_attention.1.rows_ref, bf16[8,32,2,512]{3,2,1,0:T(2,128)(2,1)S(1)} %bitcast.6, bf16[16,2,512]{2,1,0:T(2,128)(2,1)S(1)} %bitcast.8), custom_call_target="tpu_custom_call" | custom-call | tf_op jit(solution)/shard_map/finish/pallas_call | solution.py:507
Async XLA Ops:
  1.9 27.0 %copy-start = (bf16[1,8,32,2,512]{4,3,2,1,0:T(2,128)(2,1)S(1)}, bf16[1,8,32,2,512]{4,3,2,1,0:T(2,128)(2,1)}, u32[]{:S(2)}) copy-start(bf16[1,8,32,2,512]{4,3,2,1,0:T(2,128)(2,1)} %param.10) | copy-start | bytes 1572868
  1.9 27.0 %copy-start.1 = (bf16[1,16,2,512]{3,2,1,0:T(2,128)(2,1)S(1)}, bf16[1,16,2,512]{3,2,1,0:T(2,128)(2,1)}, u32[]{:S(2)}) copy-start(bf16[1,16,2,512]{3,2,1,0:T(2,128)(2,1)} %param.9) | copy-start | bytes 98308

commit v3 on v2

--- a/solution.py
+++ b/solution.py
@@ -18,12 +18,12 @@
 
 def kernel(
     n_inst, n_aa, kv_heads,
-    table_ref, len_ref, page_ref, dest_ref, q_hbm, pool_hbm, fresh_hbm,
+    table_hbm, len_hbm, page_hbm, dest_hbm, q_hbm, pool_hbm, fresh_hbm,
     out_ref,
-    q_ref, pool_ref, fresh_ref,
+    table_ref, len_ref, page_ref, dest_ref, q_ref, pool_ref, fresh_ref,
     ext, st_rn, st_out, passed, kv_mov, kv_rn, metas,
-    run_max, run_sum, run_out, q_turned,
-    s_load, s_all, r_rn, r_mov, r_peer, r_pass, r_row, r_meta, s_wide,
+    run_max, run_sum, spare_score, run_out, q_turned,
+    s_load, s_all, r_rn, r_mov, r_peer, r_pass, r_meta, s_wide,
 ):
     b = lax.axis_index("ba")
     a = lax.axis_index("aa")
@@ -70,12 +70,18 @@
     pool_load.start()
     q_load = pltpu.make_async_copy(q_hbm, q_ref, s_load.at[1])
     fresh_load = pltpu.make_async_copy(fresh_hbm, fresh_ref, s_load.at[2])
+    small = []
+    for n, (src, dst) in enumerate(((page_hbm, page_ref), (dest_hbm, dest_ref), (len_hbm, len_ref), (table_hbm, table_ref))):
+        small.append(pltpu.make_async_copy(src, dst, s_load.at[3 + n]))
+        small[-1].start()
     fresh_load.start()
     q_load.start()
 
     barrier = pltpu.get_barrier_semaphore()
-    partners = [(b, device_at[j]) for j in range(1, kv_heads)]
-    partners += [(b, peers[k]) for k in range(1, share)]
+    partners = [
+        (b, heads_at[j] * share + lax.rem(member + k, share))
+        for j in range(kv_heads) for k in range(share) if j or k
+    ]
     partners += [(near(k), to) for k in range(1, half) for to in device_at]
     partners += [(far(t), a) for t in range(half)]
     for ba, aa in partners:
@@ -84,6 +90,8 @@
     def columns_of(h):
         return slice(h * HEAD_DIM, (h + 1) * HEAD_DIM)
 
+    for load in small:
+        load.wait()
     code = len_ref[0, 0]
     for i in range(moves):
         code = code * (1 << bits) + dest_ref[0, i]
@@ -109,9 +117,9 @@
 
     pool_load.wait()
     for i in range(moves):
+        turned = jnp.swapaxes(pool_ref[page_ref[0, i]], 0, 1)
         for h in range(kv_heads):
-            for w in range(2):
-                ext[i, h, w] = pool_ref[page_ref[0, i], :, w, columns_of(h)]
+            ext[i, h] = turned[:, :, columns_of(h)]
     picked_far = [chosen_for(far(t)) for t in range(half)]
     picked_near = [chosen_for(near(k)) for k in range(half)]
     for n, (kind, t, m) in enumerate(outs):
@@ -170,11 +178,10 @@
         return count
 
     fresh_load.wait()
-    for h in range(kv_heads):
-        for w in range(2):
-            st_rn[h, w, 0:fresh, :] = fresh_ref[:, w, columns_of(h)]
-            for i in range(table):
-                st_rn[h, w, fresh + i * page_rows:fresh + (i + 1) * page_rows, :] = pool_ref[table_ref[0, i], :, w, columns_of(h)]
+    for lo, block in [(0, 0)] + [(fresh + i * page_rows, i) for i in range(table)]:
+        turned = jnp.swapaxes(fresh_ref[...] if lo == 0 else pool_ref[table_ref[0, block]], 0, 1)
+        for h in range(kv_heads):
+            st_rn[h, :, lo:lo + turned.shape[1], :] = turned[:, :, columns_of(h)]
     pl.semaphore_wait(barrier, len(partners))
 
     def source(j, lo, hi):
@@ -206,40 +213,57 @@
 
     send_on(0, 0)
     for j in range(1, kv_heads):
-        start("row", metas.at[0, 0, 0], metas.at[0, 0, j], r_row.at[0], b, device_at[j])
-    for j in range(1, kv_heads):
         send_plane(j, 0)
-    send_near(0)
     send_on(0, 1)
+    for j in range(kv_heads):
+        for k in range(share):
+            if j or k:
+                to = heads_at[j] * share + lax.rem(member + k, share)
+                kk = (share - k) % share
+                start("row", metas.at[0, 0, 0], metas.at[0, kk, j], r_meta.at[0, kk], b, to)
+    for j in range(kv_heads):
+        send_near(j)
     for j in range(1, kv_heads):
         send_plane(j, 1)
     for k in range(1, share):
         start("rows", st_rn.at[mine], kv_rn.at[share - k, 0], r_rn.at[share - k, 0], b, peers[k])
+    for j in range(1, kv_heads):
+        start("rows", st_rn.at[heads_at[j]], kv_rn.at[0, j], r_rn.at[0, j], b, device_at[j])
 
     q_load.wait()
+    scale = math.log2(math.e) / math.sqrt(HEAD_DIM)
     for h in range(heads):
-        q_turned[:, h * queries:(h + 1) * queries] = q_ref[:, h * HEAD_DIM:(h + 1) * HEAD_DIM].T
-
-    scale = math.log2(math.e) / math.sqrt(HEAD_DIM)
-
-    def attend(keys, values, bias, first):
-        turned = values.T
-        copies = BLOCK // bias.shape[1]
-        wide = jnp.concatenate([bias] * copies, axis=1) if copies > 1 else bias
+        part = slice(h * queries, (h + 1) * queries)
+        turned = q_ref[:, h * HEAD_DIM:(h + 1) * HEAD_DIM].T.astype(jnp.float32) * scale
+        high = turned.astype(jnp.bfloat16)
+        q_turned[0:HEAD_DIM, part] = high
+        q_turned[HEAD_DIM:2 * HEAD_DIM, part] = (turned - high.astype(jnp.float32)).astype(jnp.bfloat16)
+
+    def attend(keys, values, keep, hidden, bias, first):
+        left = values.T
+        if bias is None:
+            left = left * keep
+            hidden = jnp.concatenate([hidden] * (BLOCK // LANES), axis=1)
+        else:
+            bias = jnp.concatenate([bias] * (BLOCK // bias.shape[1]), axis=1)
+        both = jnp.concatenate([keys, keys], axis=1)
         for start_at in range(0, heads * queries, BLOCK):
             block = slice(start_at, start_at + BLOCK)
-            s = jnp.dot(keys, q_turned[:, block], preferred_element_type=jnp.float32)
-            s = s * scale + wide
+            s = jnp.dot(both, q_turned[:, block], preferred_element_type=jnp.float32)
+            if bias is not None:
+                s = s + bias
             top = jnp.max(s, axis=0, keepdims=True)
             if not first:
                 old = run_max[:, block]
                 top = jnp.maximum(old, top)
             w = jnp.exp2(s - top)
             total = jnp.sum(w, axis=0, keepdims=True)
+            if bias is None:
+                total = total - hidden * jnp.exp2(spare_score[:, block] - top)
             high = w.astype(jnp.bfloat16)
             low = (w - high.astype(jnp.float32)).astype(jnp.bfloat16)
-            out = jnp.dot(turned, high, preferred_element_type=jnp.float32)
-            out = out + jnp.dot(turned, low, preferred_element_type=jnp.float32)
+            out = jnp.dot(left, high, preferred_element_type=jnp.float32)
+            out = out + jnp.dot(left, low, preferred_element_type=jnp.float32)
             if not first:
                 shrink = jnp.exp2(old - top)
                 total = total + run_sum[:, block] * shrink
@@ -251,17 +275,35 @@
     def rows_of(kk, j):
         return st_rn.at[mine] if kk == 0 and j == 0 else kv_rn.at[kk, j]
 
-    place = lax.broadcasted_iota(jnp.int32, (table * page_rows, LANES), 0)
+    chunk = table * page_rows
+    place = lax.broadcasted_iota(jnp.int32, (chunk, LANES), 0)
+    lane = lax.broadcasted_iota(jnp.int32, (1, chunk), 1)
+    slot_lane = lax.broadcasted_iota(jnp.int32, (1, LANES), 1)
+    spare = st_rn[mine, 0, fresh:fresh + 16, :]
+    for start_at in range(0, heads * queries, BLOCK):
+        block = slice(start_at, start_at + BLOCK)
+        spare_score[:, block] = jnp.dot(
+            jnp.concatenate([spare, spare], axis=1), q_turned[:, block], preferred_element_type=jnp.float32
+        )[0:1]
+    spare = spare[0:1].astype(jnp.float32)
+
+    def visible(mask, keys):
+        return jnp.where(mask, keys.astype(jnp.float32), spare).astype(jnp.bfloat16)
 
     def attend_resident(spots, first=False):
-        biases = []
+        keys, values, keep = [], [], []
+        hidden = jnp.zeros((1, LANES), jnp.int32)
         for kk, j in spots:
             live = shifted(metas[0, kk, j], bits * moves)
-            biases.append(jnp.where(place < live, 0.0, NEG_LARGE))
+            rows = rows_of(kk, j)
+            keys.append(visible(place < live, rows[0, fresh:]))
+            values.append(rows[1, fresh:])
+            wide_live = jnp.concatenate([live] * (chunk // LANES), axis=1)
+            keep.append(jnp.where(lane < wide_live, 1.0, 0.0))
+            hidden = hidden + (chunk - live)
         attend(
-            jnp.concatenate([rows_of(kk, j)[0, fresh:] for kk, j in spots], axis=0),
-            jnp.concatenate([rows_of(kk, j)[1, fresh:] for kk, j in spots], axis=0),
-            jnp.concatenate(biases, axis=0), first,
+            jnp.concatenate(keys, axis=0), jnp.concatenate(values, axis=0),
+            jnp.concatenate(keep, axis=1).astype(jnp.bfloat16), hidden.astype(jnp.float32), None, first,
         )
 
     def attend_fresh():
@@ -275,18 +317,26 @@
         attend(
             jnp.concatenate([rows_of(kk, j)[0, :fresh] for kk, j in spots], axis=0),
             jnp.concatenate([rows_of(kk, j)[1, :fresh] for kk, j in spots], axis=0),
-            jnp.concatenate(biases, axis=0), False,
+            None, None, jnp.concatenate(biases, axis=0), False,
         )
 
     def attend_moved(spots):
-        biases = []
-        for i, kk, j, m in spots:
+        along = LANES // page_rows
+        keys, keep = [], []
+        hidden = jnp.zeros((1, LANES), jnp.float32)
+        for n, (i, kk, j, m) in enumerate(spots):
             count = taken(metas[1 + i, kk, j], b)
-            biases.append(jnp.broadcast_to(jnp.where(count > m, 0.0, NEG_LARGE), (page_rows, LANES)))
+            keys.append(visible(jnp.broadcast_to(count, (page_rows, LANES)) > m, kv_mov[i, kk, j, m, 0]))
+            used = jnp.where(count > m, 1.0, 0.0)
+            hidden = hidden + (1.0 - used) * page_rows
+            if n % along == 0:
+                keep.append(used)
+            else:
+                keep[-1] = jnp.where(slot_lane >= n % along * page_rows, used, keep[-1])
         attend(
-            jnp.concatenate([kv_mov[i, kk, j, m, 0] for i, kk, j, m in spots], axis=0),
+            jnp.concatenate(keys, axis=0),
             jnp.concatenate([kv_mov[i, kk, j, m, 1] for i, kk, j, m in spots], axis=0),
-            jnp.concatenate(biases, axis=0), False,
+            jnp.concatenate(keep, axis=1).astype(jnp.bfloat16), hidden, None, False,
         )
 
     members = range(share)
@@ -337,15 +387,13 @@
                     start("leaf", spot, kv_mov.at[i, share - p, j, 1], r_peer.at[i, share - p - 1, 1], b, peers[p])
 
     def send_metas():
-        arrived(metas.at[0, 0, 1:kv_heads], r_row.at[0])
+        arrived(metas.at[0, 0, 1:kv_heads], r_meta.at[0, 0])
         block = metas.at[0, 0]
         for t in range(half):
             g = 1 + near_count + reach
             start("block", block, metas.at[g, 0], r_meta.at[g, 0], far(t), a)
         for k in range(1, half):
             start("block", block, metas.at[k, 0], r_meta.at[k, 0], near(k), a)
-        for p in range(1, share):
-            start("block", block, metas.at[0, share - p], r_meta.at[0, share - p], b, peers[p])
 
     def relay_metas():
         for g in range(1, groups):
@@ -355,25 +403,28 @@
 
     def peers_metas(lo, hi):
         for kk in range(1, share):
-            arrived(metas.at[lo:hi, kk], r_meta.at[lo, kk])
-
-    def do_resident(j):
-        peers_rows(j)
-        attend_resident([(kk, j) for kk in members])
-
-    def do_near(part):
+            arrived(metas.at[lo:hi, kk] if lo else metas.at[0, kk], r_meta.at[lo, kk])
+
+    def attend_near(part):
+        js = list(chips)[2 * part:2 * part + 2]
+        for k in range(near_count):
+            attend_moved([(k, kk, j, m) for j in js for kk in members for m in slots])
+
+    def peers_near(part):
         js = list(chips)[2 * part:2 * part + 2]
         for k in range(near_count):
             for kk in range(1, share):
                 arrived(kv_mov.at[k, kk, js[0]:js[-1] + 1], r_peer.at[k, kk - 1, part])
-            attend_moved([(k, kk, j, m) for j in js for kk in members for m in slots])
-
-    def do_far(e, m):
+
+    def peers_far(e, m):
         i = near_count + e
         for kk in range(1, share):
             arrived(kv_mov.at[i, kk, :, m], r_peer.at[i, kk - 1, m])
-        attend_moved([(i, kk, j, m) for j in chips for kk in members])
-
+
+    def attend_far(e, m):
+        attend_moved([(near_count + e, kk, j, m) for j in chips for kk in members])
+
+    others = range(1, kv_heads)
     late = [m for m in reversed(slots) if m == 0 or not shared]
 
     def relay_late(j):
@@ -381,53 +432,60 @@
             for m in late:
                 relay_far(e, j, m)
 
-    attend_resident([(0, 0)], True)
     send_on(1, 0)
     send_on(2, 0)
+    peers_metas(0, 1)
+    peers_rows(0)
+    attend_resident([(kk, 0) for kk in members], True)
+    send_on(3, 0)
     send_metas()
-    peers_metas(0, 1)
-    send_on(3, 0)
     send_on(1, 1)
     send_on(2, 1)
-    for j in range(1, kv_heads):
-        send_near(j)
-    peers_rows(0)
-    attend_resident([(kk, 0) for kk in range(1, share)])
+    send_on(3, 1)
     if shared:
-        hub_relay([(0, 0), (1, 0), (0, 1)])
-    send_on(3, 1)
-    for j in range(1, kv_heads):
-        start("rows", st_rn.at[heads_at[j]], kv_rn.at[0, j], r_rn.at[0, j], b, device_at[j])
-    relay_metas()
-    if shared:
-        hub_relay([(0, 2), (0, 3), (1, 1)])
+        hub_relay([(0, 0), (1, 0), (0, 1), (0, 2)])
     relay_near(0)
     relay_late(0)
+    relay_near(1)
     if shared:
-        hub_relay([(1, 2), (1, 3)])
-    relay_near(1)
+        hub_relay([(0, 3), (1, 1), (1, 2)])
+    relay_near(2)
+    relay_near(3)
+    relay_rows(1)
+    relay_metas()
+    relay_rows(2)
+    if shared:
+        hub_relay([(1, 3)])
+    peers_near(0)
+    peers_near(1)
     peers_metas(1, groups)
-    do_near(0)
-    relay_rows(1)
-    relay_rows(2)
-    relay_near(2)
+    attend_near(0)
+    attend_near(1)
+    relay_rows(3)
     relay_late(1)
-    do_resident(1)
-    relay_rows(3)
-    relay_near(3)
-    do_resident(2)
+    peers_rows(1)
+    peers_rows(2)
+    attend_resident([(kk, 1) for kk in members])
+    attend_resident([(kk, 2) for kk in members])
     relay_late(2)
-    do_near(1)
-    do_resident(3)
+    peers_rows(3)
     relay_late(3)
+    if shared:
+        leaf_relay([(0, j) for j in chips])
+    attend_resident([(kk, 3) for kk in members])
     attend_fresh()
     if shared:
-        leaf_relay([(e, j) for j in chips for e in range(half)])
-        do_far(0, 1)
-        do_far(1, 1)
+        leaf_relay([(e, j) for e in range(1, half) for j in chips])
+        peers_far(0, 1)
+        peers_far(1, 1)
+        attend_far(0, 1)
+        attend_far(1, 1)
     for m in late:
         for e in range(half):
-            do_far(e, m)
+            peers_far(e, m)
+    for m in late:
+        for e in range(half):
+            attend_far(e, m)
 
     def turn(h):
         part = slice(h * queries, (h + 1) * queries)
@@ -480,9 +538,10 @@
     attended = pl.pallas_call(
         functools.partial(kernel, n_inst, n_aa, kv_heads),
         out_shape=pltpu.VMEM((query_count, q_width), bf),
-        in_specs=[pl.BlockSpec(memory_space=pltpu.SMEM)] * 4 + [pl.BlockSpec(memory_space=pltpu.HBM)] * 3,
+        in_specs=[pl.BlockSpec(memory_space=pltpu.HBM)] * 7,
         out_specs=pl.BlockSpec(memory_space=pltpu.VMEM),
         scratch_shapes=[
+            *[pltpu.SMEM(x.shape, jnp.int32) for x in (page_table, ctx_len, move_page, move_dest)],
             pltpu.VMEM((query_count, q_width), bf),
             pltpu.VMEM(pool_pages.shape, bf),
             pltpu.VMEM(fresh_rows.shape, bf),
@@ -495,11 +554,12 @@
             pltpu.VMEM((groups, share, kv_heads, 1, LANES), jnp.int32),
             pltpu.VMEM((1, heads * query_count), f32),
             pltpu.VMEM((1, heads * query_count), f32),
+            pltpu.VMEM((1, heads * query_count), f32),
             pltpu.VMEM((HEAD_DIM, heads * query_count), f32),
-            pltpu.VMEM((HEAD_DIM, heads * query_count), bf),
-            dma((3,)), dma((7, per_kind)),
+            pltpu.VMEM((2 * HEAD_DIM, heads * query_count), bf),
+            dma((7,)), dma((7, per_kind)),
             dma((share, kv_heads)), dma((near + half, kv_heads, MOST)), dma((near + half, share - 1, MOST)),
-            dma((kv_heads, 2)), dma((1,)), dma((groups, share)), dma((kv_heads, 2) if half > 2 else (1, 1)),
+            dma((kv_heads, 2)), dma((groups, share)), dma((kv_heads, 2) if half > 2 else (1, 1)),
         ],
         compiler_params=pltpu.CompilerParams(collective_id=0, has_side_effects=True, vmem_limit_bytes=60 * 2**20),
         name="paged_attention",

time: 30.1 us -> 27.5 us (0.914)
  Pallas kernels: 27.9 us -> 25.4 us
    pallas_call x1, Pallas kernels: 27 us -> 24.4 us  [local(): pl.pallas_call(functools.partial(kernel, n_inst, n_aa, kv_heads), out_sha...]
where the time goes in v3:
time: 27.5 us; the launch traced here: 27.3 us
  Pallas kernels  25.4 us (92%)
  between operations  1.96 us (7%)
    pallas_call x1, Pallas kernels, local(): pl.pallas_call(functools.partial(kernel, n_inst, n_aa, kv_heads), out_sha...  24.4 us
    pallas_call x1, Pallas kernels, local(): pl.pallas_call(finish, out_shape=(jax.ShapeDtypeStruct(attended.shape, bf...  0.94 us

profile of v3, /device:TPU:0, one launch (start us, length us, event | category | flops | bytes accessed | tf_op | source)
XLA Modules:
  0.0 27.3 jit_solution(16168478061937250693)
XLA Ops:
  1.9 0.0 copy-start
  1.9 0.0 copy-start.1
  1.9 24.4 %paged_attention.1.rows_ref = bf16[128,1024]{1,0:T(8,128)(2,1)S(1)} custom-call(s32[1,4]{1,0:T(1,128)} %table_hbm.1, s32[1,1]{1,0:T(1,128)S(6)} %copy.10.len_hbm, s32[1,3]{1,0:T(1,128)} %page_hbm.1, s32[1,3]{1,0:T(1,128)} %dest_hbm.1, bf16[128,1024]{1,0:T(8,128)(2,1)} %bitcast.9, bf16[8,32,2,512]{3,2,1,0:T(2,128)(2,1)} %bitcast.5, bf16[16,2,512]{2,1,0:T(2,128)(2,1)} %bitcast.7), custom_call_target="tpu_custom_call" | custom-call | tf_op jit(solution)/shard_map/paged_attention/pallas_call | solution.py:538
  26.4 0.0 copy-done
  26.4 0.0 copy-done.1
  26.4 0.9 %finish.1 = (bf16[128,1024]{1,0:T(8,128)(2,1)}, bf16[8,32,2,512]{3,2,1,0:T(2,128)(2,1)}) custom-call(s32[1,1]{1,0:T(1,128)S(6)} %copy.11.append_ref, bf16[128,1024]{1,0:T(8,128)(2,1)S(1)} %paged_attention.1.rows_ref, bf16[8,32,2,512]{3,2,1,0:T(2,128)(2,1)S(1)} %bitcast.6, bf16[16,2,512]{2,1,0:T(2,128)(2,1)S(1)} %bitcast.8), custom_call_target="tpu_custom_call" | custom-call | tf_op jit(solution)/shard_map/finish/pallas_call | solution.py:567
Async XLA Ops:
  1.9 24.5 %copy-start = (bf16[1,8,32,2,512]{4,3,2,1,0:T(2,128)(2,1)S(1)}, bf16[1,8,32,2,512]{4,3,2,1,0:T(2,128)(2,1)}, u32[]{:S(2)}) copy-start(bf16[1,8,32,2,512]{4,3,2,1,0:T(2,128)(2,1)} %param.10) | copy-start | bytes 1572868
  1.9 24.5 %copy-start.1 = (bf16[1,16,2,512]{3,2,1,0:T(2,128)(2,1)S(1)}, bf16[1,16,2,512]{3,2,1,0:T(2,128)(2,1)}, u32[]{:S(2)}) copy-start(bf16[1,16,2,512]{3,2,1,0:T(2,128)(2,1)} %param.9) | copy-start | bytes 98308

commit v4 on v3

--- a/solution.py
+++ b/solution.py
@@ -78,10 +78,8 @@
     q_load.start()
 
     barrier = pltpu.get_barrier_semaphore()
-    partners = [
-        (b, heads_at[j] * share + lax.rem(member + k, share))
-        for j in range(kv_heads) for k in range(share) if j or k
-    ]
+    partners = [(b, device_at[j]) for j in range(1, kv_heads)]
+    partners += [(b, peers[k]) for k in range(1, share)]
     partners += [(near(k), to) for k in range(1, half) for to in device_at]
     partners += [(far(t), a) for t in range(half)]
     for ba, aa in partners:
@@ -146,6 +144,7 @@
         "rows": (kv_heads, lambda r: st_rn.at[0:r]),
         "row": (kv_heads, lambda r: metas.at[0, 0, 0:r]),
         "block": (groups, lambda r: metas.at[0:r, 0]),
+        "part": (groups, lambda r: metas.at[0:r, 0, 1:kv_heads]),
     }
     names = list(kinds)
     counts = {name: 0 for name in names}
@@ -215,12 +214,10 @@
     for j in range(1, kv_heads):
         send_plane(j, 0)
     send_on(0, 1)
-    for j in range(kv_heads):
-        for k in range(share):
-            if j or k:
-                to = heads_at[j] * share + lax.rem(member + k, share)
-                kk = (share - k) % share
-                start("row", metas.at[0, 0, 0], metas.at[0, kk, j], r_meta.at[0, kk], b, to)
+    for j in range(1, kv_heads):
+        start("row", metas.at[0, 0, 0], metas.at[0, 0, j], r_meta.at[0, 0], b, device_at[j])
+    for k in range(1, share):
+        start("row", metas.at[0, 0, 0], metas.at[0, share - k, 0], r_meta.at[0, share - k], b, peers[k])
     for j in range(kv_heads):
         send_near(j)
     for j in range(1, kv_heads):
@@ -394,16 +391,26 @@
             start("block", block, metas.at[g, 0], r_meta.at[g, 0], far(t), a)
         for k in range(1, half):
             start("block", block, metas.at[k, 0], r_meta.at[k, 0], near(k), a)
-
-    def relay_metas():
-        for g in range(1, groups):
+        for p in range(1, share):
+            start("part", metas.at[0, 0, 1:kv_heads], metas.at[0, share - p, 1:kv_heads], r_meta.at[groups, share - p], b, peers[p])
+
+    def relay_metas(lo, hi):
+        for g in range(lo, hi):
             arrived(metas.at[g, 0], r_meta.at[g, 0])
             for p in range(1, share):
-                start("block", metas.at[g, 0], metas.at[g, share - p], r_meta.at[1, share - p], b, peers[p])
+                start("block", metas.at[g, 0], metas.at[g, share - p], r_meta.at[lo, share - p], b, peers[p])
+
+    def peers_own_row():
+        for kk in range(1, share):
+            arrived(metas.at[0, kk, 0], r_meta.at[0, kk])
+
+    def peers_plane():
+        for kk in range(1, share):
+            arrived(metas.at[0, kk, 1:kv_heads], r_meta.at[groups, kk])
 
     def peers_metas(lo, hi):
         for kk in range(1, share):
-            arrived(metas.at[lo:hi, kk] if lo else metas.at[0, kk], r_meta.at[lo, kk])
+            arrived(metas.at[lo:hi, kk], r_meta.at[lo, kk])
 
     def attend_near(part):
         js = list(chips)[2 * part:2 * part + 2]
@@ -434,7 +441,7 @@
 
     send_on(1, 0)
     send_on(2, 0)
-    peers_metas(0, 1)
+    peers_own_row()
     peers_rows(0)
     attend_resident([(kk, 0) for kk in members], True)
     send_on(3, 0)
@@ -442,49 +449,52 @@
     send_on(1, 1)
     send_on(2, 1)
     send_on(3, 1)
+    first_far = 1 + near_count
     if shared:
-        hub_relay([(0, 0), (1, 0), (0, 1), (0, 2)])
+        hub_relay([(0, 0), (1, 0), (0, 1)])
+    if near_count:
+        relay_metas(1, first_far)
     relay_near(0)
+    relay_near(1)
     relay_late(0)
-    relay_near(1)
     if shared:
-        hub_relay([(0, 3), (1, 1), (1, 2)])
+        hub_relay([(0, 2), (0, 3)])
+    if near_count:
+        peers_metas(1, first_far)
+    peers_near(0)
+    attend_near(0)
     relay_near(2)
     relay_near(3)
+    if shared:
+        hub_relay([(1, 1), (1, 2)])
     relay_rows(1)
-    relay_metas()
     relay_rows(2)
+    peers_near(1)
+    attend_near(1)
+    relay_rows(3)
     if shared:
         hub_relay([(1, 3)])
-    peers_near(0)
-    peers_near(1)
-    peers_metas(1, groups)
-    attend_near(0)
-    attend_near(1)
-    relay_rows(3)
     relay_late(1)
+    peers_plane()
     peers_rows(1)
     peers_rows(2)
     attend_resident([(kk, 1) for kk in members])
     attend_resident([(kk, 2) for kk in members])
     relay_late(2)
-    peers_rows(3)
+    relay_metas(first_far, groups)
     relay_late(3)
     if shared:
         leaf_relay([(0, j) for j in chips])
+    peers_rows(3)
     attend_resident([(kk, 3) for kk in members])
     attend_fresh()
     if shared:
         leaf_relay([(e, j) for e in range(1, half) for j in chips])
-        peers_far(0, 1)
-        peers_far(1, 1)
-        attend_far(0, 1)
-        attend_far(1, 1)
-    for m in late:
-        for e in range(half):
+    peers_metas(first_far, groups)
+    for e in range(half):
+        for m in reversed(slots):
             peers_far(e, m)
-    for m in late:
-        for e in range(half):
+        for m in reversed(slots):
             attend_far(e, m)
 
     def turn(h):
@@ -557,9 +567,9 @@
             pltpu.VMEM((1, heads * query_count), f32),
             pltpu.VMEM((HEAD_DIM, heads * query_count), f32),
             pltpu.VMEM((2 * HEAD_DIM, heads * query_count), bf),
-            dma((7,)), dma((7, per_kind)),
+            dma((7,)), dma((8, per_kind)),
             dma((share, kv_heads)), dma((near + half, kv_heads, MOST)), dma((near + half, share - 1, MOST)),
-            dma((kv_heads, 2)), dma((groups, share)), dma((kv_heads, 2) if half > 2 else (1, 1)),
+            dma((kv_heads, 2)), dma((groups + 1, share)), dma((kv_heads, 2) if half > 2 else (1, 1)),
         ],
         compiler_params=pltpu.CompilerParams(collective_id=0, has_side_effects=True, vmem_limit_bytes=60 * 2**20),
         name="paged_attention",

time: 27.5 us -> 25.4 us (0.924)
  Pallas kernels: 25.4 us -> 23.3 us
    pallas_call x1, Pallas kernels: 24.4 us -> 22.4 us  [local(): pl.pallas_call(functools.partial(kernel, n_inst, n_aa, kv_heads), out_sha...]
where the time goes in v4:
time: 25.4 us; the launch traced here: 25.3 us
  Pallas kernels  23.3 us (92%)
  between operations  1.96 us (8%)
    pallas_call x1, Pallas kernels, local(): pl.pallas_call(functools.partial(kernel, n_inst, n_aa, kv_heads), out_sha...  22.4 us
    pallas_call x1, Pallas kernels, local(): pl.pallas_call(finish, out_shape=(jax.ShapeDtypeStruct(attended.shape, bf...  0.94 us

profile of v4, /device:TPU:0, one launch (start us, length us, event | category | flops | bytes accessed | tf_op | source)
XLA Modules:
  0.0 25.3 jit_solution(13764079267164759250)
XLA Ops:
  1.9 0.0 copy-start
  1.9 0.0 copy-start.1
  1.9 22.4 %paged_attention.1.rows_ref = bf16[128,1024]{1,0:T(8,128)(2,1)S(1)} custom-call(s32[1,4]{1,0:T(1,128)} %table_hbm.1, s32[1,1]{1,0:T(1,128)S(6)} %copy.10.len_hbm, s32[1,3]{1,0:T(1,128)} %page_hbm.1, s32[1,3]{1,0:T(1,128)} %dest_hbm.1, bf16[128,1024]{1,0:T(8,128)(2,1)} %bitcast.9, bf16[8,32,2,512]{3,2,1,0:T(2,128)(2,1)} %bitcast.5, bf16[16,2,512]{2,1,0:T(2,128)(2,1)} %bitcast.7), custom_call_target="tpu_custom_call" | custom-call | tf_op jit(solution)/shard_map/paged_attention/pallas_call | solution.py:548
  24.3 0.0 copy-done
  24.3 0.0 copy-done.1
  24.3 0.9 %finish.1 = (bf16[128,1024]{1,0:T(8,128)(2,1)}, bf16[8,32,2,512]{3,2,1,0:T(2,128)(2,1)}) custom-call(s32[1,1]{1,0:T(1,128)S(6)} %copy.11.append_ref, bf16[128,1024]{1,0:T(8,128)(2,1)S(1)} %paged_attention.1.rows_ref, bf16[8,32,2,512]{3,2,1,0:T(2,128)(2,1)S(1)} %bitcast.6, bf16[16,2,512]{2,1,0:T(2,128)(2,1)S(1)} %bitcast.8), custom_call_target="tpu_custom_call" | custom-call | tf_op jit(solution)/shard_map/finish/pallas_call | solution.py:577
Async XLA Ops:
  1.9 22.4 %copy-start = (bf16[1,8,32,2,512]{4,3,2,1,0:T(2,128)(2,1)S(1)}, bf16[1,8,32,2,512]{4,3,2,1,0:T(2,128)(2,1)}, u32[]{:S(2)}) copy-start(bf16[1,8,32,2,512]{4,3,2,1,0:T(2,128)(2,1)} %param.10) | copy-start | bytes 1572868
  1.9 22.4 %copy-start.1 = (bf16[1,16,2,512]{3,2,1,0:T(2,128)(2,1)S(1)}, bf16[1,16,2,512]{3,2,1,0:T(2,128)(2,1)}, u32[]{:S(2)}) copy-start(bf16[1,16,2,512]{3,2,1,0:T(2,128)(2,1)} %param.9) | copy-start | bytes 98308

commit v5 on v4

--- a/solution.py
+++ b/solution.py
@@ -458,22 +458,18 @@
     relay_near(1)
     relay_late(0)
     if shared:
-        hub_relay([(0, 2), (0, 3)])
+        hub_relay([(0, 2), (1, 1), (0, 3), (1, 2), (1, 3)])
     if near_count:
         peers_metas(1, first_far)
     peers_near(0)
     attend_near(0)
     relay_near(2)
     relay_near(3)
-    if shared:
-        hub_relay([(1, 1), (1, 2)])
     relay_rows(1)
     relay_rows(2)
     peers_near(1)
     attend_near(1)
     relay_rows(3)
-    if shared:
-        hub_relay([(1, 3)])
     relay_late(1)
     peers_plane()
     peers_rows(1)
@@ -540,7 +536,7 @@
     near = half - 1
     groups = 1 + near + half
     out_count = (near + half) * MOST
-    per_kind = 3 if share < 4 else 9
+    per_kind = 2 if share < 4 else 9
     bf, f32 = jnp.bfloat16, jnp.float32
     dma = pltpu.SemaphoreType.DMA
     page = (2, page_rows, HEAD_DIM)

time: 25.4 us -> 25 us (0.984)
  Pallas kernels: 23.3 us -> 22.8 us
    pallas_call x1, Pallas kernels: 22.4 us -> 21.9 us  [local(): pl.pallas_call(functools.partial(kernel, n_inst, n_aa, kv_heads), out_sha...]
where the time goes in v5:
time: 25 us; the launch traced here: 24.8 us
  Pallas kernels  22.8 us (91%)
  between operations  1.96 us (8%)
    pallas_call x1, Pallas kernels, local(): pl.pallas_call(functools.partial(kernel, n_inst, n_aa, kv_heads), out_sha...  21.9 us
    pallas_call x1, Pallas kernels, local(): pl.pallas_call(finish, out_shape=(jax.ShapeDtypeStruct(attended.shape, bf...  0.94 us

profile of v5, /device:TPU:0, one launch (start us, length us, event | category | flops | bytes accessed | tf_op | source)
XLA Modules:
  0.0 24.8 jit_solution(13107865426189511356)
XLA Ops:
  1.9 0.0 copy-start
  1.9 0.0 copy-start.1
  1.9 21.9 %paged_attention.1.rows_ref = bf16[128,1024]{1,0:T(8,128)(2,1)S(1)} custom-call(s32[1,4]{1,0:T(1,128)} %table_hbm.1, s32[1,1]{1,0:T(1,128)S(6)} %copy.10.len_hbm, s32[1,3]{1,0:T(1,128)} %page_hbm.1, s32[1,3]{1,0:T(1,128)} %dest_hbm.1, bf16[128,1024]{1,0:T(8,128)(2,1)} %bitcast.9, bf16[8,32,2,512]{3,2,1,0:T(2,128)(2,1)} %bitcast.5, bf16[16,2,512]{2,1,0:T(2,128)(2,1)} %bitcast.7), custom_call_target="tpu_custom_call" | custom-call | tf_op jit(solution)/shard_map/paged_attention/pallas_call | solution.py:544
  23.9 0.0 copy-done
  23.9 0.0 copy-done.1
  23.9 0.9 %finish.1 = (bf16[128,1024]{1,0:T(8,128)(2,1)}, bf16[8,32,2,512]{3,2,1,0:T(2,128)(2,1)}) custom-call(s32[1,1]{1,0:T(1,128)S(6)} %copy.11.append_ref, bf16[128,1024]{1,0:T(8,128)(2,1)S(1)} %paged_attention.1.rows_ref, bf16[8,32,2,512]{3,2,1,0:T(2,128)(2,1)S(1)} %bitcast.6, bf16[16,2,512]{2,1,0:T(2,128)(2,1)S(1)} %bitcast.8), custom_call_target="tpu_custom_call" | custom-call | tf_op jit(solution)/shard_map/finish/pallas_call | solution.py:573
Async XLA Ops:
  1.9 21.9 %copy-start = (bf16[1,8,32,2,512]{4,3,2,1,0:T(2,128)(2,1)S(1)}, bf16[1,8,32,2,512]{4,3,2,1,0:T(2,128)(2,1)}, u32[]{:S(2)}) copy-start(bf16[1,8,32,2,512]{4,3,2,1,0:T(2,128)(2,1)} %param.10) | copy-start | bytes 1572868
  1.9 21.9 %copy-start.1 = (bf16[1,16,2,512]{3,2,1,0:T(2,128)(2,1)S(1)}, bf16[1,16,2,512]{3,2,1,0:T(2,128)(2,1)}, u32[]{:S(2)}) copy-start(bf16[1,16,2,512]{3,2,1,0:T(2,128)(2,1)} %param.9) | copy-start | bytes 98308
